TPU v7x, 32 devices: a whole 2x2x4 slice. The times are simulated.
32 devices in a mesh: role: 2 (over core), rep: 4 (over z), tp: 4 (over y, x).
Axes of the slice: x: 2, y: 2, z: 4, core: 2. Of those that a mesh axis runs over, the one named last changes fastest.
Arguments:
- pre_act: bfloat16 [2, 2, 64, 14784], P('role', None, 'rep', 'tp'), may hold values from -6 to 6
- next_pre: bfloat16 [2, 2, 64, 14784], P('role', None, 'rep', 'tp'), may hold values from -6 to 6
- stream: bfloat16 [2, 2, 64, 8192], P('role', None, 'tp', 'rep'), may hold values from -6 to 6
- cotangent: bfloat16 [64, 8192], P('tp', 'rep'), may hold values from -6 to 6
- weights: float32 [2, 14784, 8192], P('role', 'tp', 'rep'), may hold values from -6 to 6
- first_moment: float32 [14784, 8192], P('tp', 'rep'), may hold values from -0.18 to 0.18
- second_moment: float32 [14784, 8192], P('tp', 'rep'), may hold values from 0.0001 to 0.001
- tree_parent: int32 [2, 64], P('role', 'tp'), may hold values from 0 to 63, as said below
- tree_depth: int32 [2, 64], P('role', 'tp'), may hold values from 1 to 16, as said below
Outputs:
- first_out: bfloat16 [2, 64, 8192], P('role', 'tp', 'rep')
- next_out: bfloat16 [2, 64, 8192], P('role', 'tp', 'rep')
- new_weights: float32 [2, 14784, 8192], P('role', 'tp', 'rep')
Inputs may be any that keep to these rules, and one draw needn't show every extreme that they name: `tree_parent`: each entry names a first-pass row of the same group that lies in the same aligned block of 16 rows as the entry's own row. `tree_depth`: one more than the depth of the named parent in its block's first-pass tree; in that tree every row but the block's first names an earlier row of the block as parent, and the first row has depth 0.
All inputs are finite; a program needn't handle non-finite values.
Results may differ from a plain program's by a relative error of at most 0.0041.
Values may be sent and summed in bfloat16 or wider, within the bound.
No kernel may reach another device: no remote copies, remote signals or barrier semaphores. Data moves between devices by JAX's collectives and lax.ppermute only.
A program may use at most 256 MiB of HBM per device.

v0:
```python
import jax
import jax.numpy as jnp
from jax import lax
from jax.sharding import PartitionSpec as P

FF = 14784


beta_one = 0.9
beta_two = 0.95
epsilon = 1e-08
learn_rate = 0.08
decay_rate = 0.1
correct_one = 1.0 - 0.9**60
correct_two = 1.0 - 0.95**60


def shifted(value, axis, by):
    size = lax.axis_size(axis)
    pairs = [(i, i + by) for i in range(size) if 0 <= i + by < size]
    return lax.ppermute(value, axis, pairs)


def activate(both_halves):
    return (
        jax.nn.silu(both_halves[0].astype(jnp.float32)) * both_halves[1].astype(jnp.float32)
    ).astype(jnp.bfloat16)


def adam_step(master, moment_one, moment_two, gradient):
    moment_one = beta_one * moment_one + (1.0 - beta_one) * gradient
    moment_two = beta_two * moment_two + (1.0 - beta_two) * gradient * gradient
    direction = moment_one / correct_one / (jnp.sqrt(moment_two / correct_two) + epsilon)
    return master - learn_rate * (direction + decay_rate * master)


def local(
    pre_act,
    next_pre,
    stream,
    cotangent,
    weights,
    first_moment,
    second_moment,
    tree_parent,
    tree_depth,
):
    learner = lax.axis_index("role") == 0
    factor = FF ** (-0.5)
    hidden = activate(pre_act[0])
    upcoming = activate(next_pre[0])
    older = weights[0].astype(jnp.bfloat16)
    cot_rows = lax.all_gather(cotangent, "tp", axis=0, tiled=True)
    width_ff, width_d = older.shape
    empty_grad = jnp.zeros((width_ff, width_d), jnp.float32)
    gradient = empty_grad
    segment = lax.all_gather(hidden, "rep", axis=0, tiled=True)
    piece = segment
    contribute_partial_value = piece

    def accumulate(held_sum):
        return lax.dot_general(
            segment, cot_rows, (((0,), (0,)), ((), ())), preferred_element_type=jnp.float32
        )

    gradient = lax.cond(learner, accumulate, lambda held_sum: held_sum, gradient)
    partial_value, gradient = (contribute_partial_value, gradient)
    summed = lax.psum_scatter(
        jnp.dot(partial_value, older, preferred_element_type=jnp.float32),
        "tp",
        scatter_dimension=0,
        tiled=True,
    )
    first_out = (stream[0, 0].astype(jnp.float32) + factor * summed).astype(jnp.bfloat16)
    updated = adam_step(weights[0], first_moment, second_moment, factor * gradient)
    fresh = updated.astype(jnp.bfloat16)
    pushed = shifted(fresh, "role", 1)
    current = jnp.where(learner, fresh, pushed)
    new_weights = jnp.where(learner, updated, pushed.astype(jnp.float32))
    piece = lax.all_gather(upcoming, "rep", axis=0, tiled=True)
    next_summed = lax.psum_scatter(
        jnp.dot(piece, current, preferred_element_type=jnp.float32),
        "tp",
        scatter_dimension=0,
        tiled=True,
    )
    block_rows = first_out.shape[0]
    local_parent = tree_parent[0] - lax.axis_index("tp") * block_rows
    onehot = (local_parent[:, None] == jnp.arange(block_rows, dtype=jnp.int32)[None, :]).astype(
        jnp.bfloat16
    )
    picked = jnp.dot(onehot, first_out, preferred_element_type=jnp.float32)
    portion = 1.0 / (1.0 + tree_depth[0].astype(jnp.float32))
    total = stream[0, 1].astype(jnp.float32) + factor * next_summed + picked * portion[:, None]
    next_out = total.astype(jnp.bfloat16)
    return (first_out[None], next_out[None], new_weights[None])


def solution(mesh):
    placed = (
        P("role", None, "rep", "tp"),
        P("role", None, "rep", "tp"),
        P("role", None, "tp", "rep"),
        P("tp", "rep"),
        P("role", "tp", "rep"),
        P("tp", "rep"),
        P("tp", "rep"),
        P("role", "tp"),
        P("role", "tp"),
    )
    return jax.shard_map(
        local,
        mesh=mesh,
        in_specs=placed,
        out_specs=(P("role", "tp", "rep"), P("role", "tp", "rep"), P("role", "tp", "rep")),
        check_vma=False,
    )
```

profile of v0, /device:TPU:0, one launch (start us, length us, event | category | flops | bytes accessed | tf_op | source)
XLA Modules:
  0.0 193.4 jit_solution(9640457482474888950)
XLA Ops:
  7.2 0.0 reduce-scatter.3.cloned.1.call-start
  7.2 1.0 fusion.15
  8.3 16.9 %all_gather.9 = bf16[64,3696]{1,0:T(8,128)(2,1)S(1)} all-gather(bf16[16,3696]{1,0:T(8,128)(2,1)S(1)} %fusion.15), channel_id=1, replica_groups=mesh['role'=2,'rep'=4,'tp'=4] {'rep'}, dimensions={0}, use_global_device_ids=true | all-gather | bytes 591360 | tf_op jit(solution)/shard_map/all_gather | solution.py:57
  25.2 9.3 %all_gather.11 = bf16[64,2048]{1,0:T(8,128)(2,1)S(1)} all-gather(bf16[16,2048]{1,0:T(8,128)(2,1)} %param.14), channel_id=1, replica_groups=mesh['role'=2,'rep'=4,'tp'=4] {'tp'}, dimensions={0}, use_global_device_ids=true | all-gather | bytes 327680 | tf_op jit(solution)/shard_map/all_gather | solution.py:53
  34.5 12.8 %conditional.1 = (f32[3696,2048]{1,0:T(8,128)}) conditional(s32[]{:T(128)} %convert_element_type.85, () %tuple.14, (bf16[64,3696]{1,0:T(8,128)(2,1)S(1)}, bf16[64,2048]{1,0:T(8,128)(2,1)S(1)}) %tuple.15), branch_computations={%region_1.2_spmd, %region_2.3_spmd} | conditional | flops 968884224 | bytes 31012872 | solution.py:66
  34.5 12.8 %fusion.28 = f32[3696,2048]{1,0:T(8,128)} fusion(bf16[64,3696]{1,0:T(8,128)(2,1)S(1)} %get-tuple-element.4, bf16[64,2048]{1,0:T(8,128)(2,1)S(1)} %get-tuple-element.8), kind=kOutput, calls=%fused_computation.39 | convolution fusion | flops 968884224 | bytes 31012864 | tf_op jit(solution)/shard_map/cond/branch_1_fun/dot_general | solution.py:62
  47.3 54.7 %fusion.24 = (bf16[3696,2048]{1,0:T(8,128)(2,1)}, f32[3696,2048]{1,0:T(8,128)}) fusion(f32[3696,2048]{1,0:T(8,128)} %get-tuple-element.16, f32[3696,2048]{1,0:T(8,128)} %param.17, f32[3696,2048]{1,0:T(8,128)} %param.16, f32[1,3696,2048]{2,1,0:T(8,128)} %param.15), kind=kLoop, calls=%fused_computation.36 | loop fusion | flops 128679936 | bytes 166526976 | tf_op jit(solution)/shard_map/convert_element_type | solution.py:76
  101.9 0.0 copy-start.2
  101.9 0.0 copy-start.3
  101.9 0.0 copy-start.4
  101.9 0.0 copy-start.1
  101.9 6.8 %collective-permute-start = (bf16[3696,2048]{1,0:T(8,128)(2,1)}, bf16[3696,2048]{1,0:T(8,128)(2,1)}, u32[]{:S(2)}, u32[]{:S(2)}) collective-permute-start(bf16[3696,2048]{1,0:T(8,128)(2,1)} %get-tuple-element.12), channel_id=1, source_target_pairs={{0,16},{1,17},{2,18},{3,19},{4,20},{5,21},{6,22},{7,23},{8,24},{9,... | collective-permute-start | bytes 45416456 | tf_op jit(solution)/shard_map/ppermute | solution.py:21
  108.7 13.1 %fusion.25 = f32[64,2048]{1,0:T(8,128)} fusion(bf16[64,3696]{1,0:T(8,128)(2,1)S(1)} %all_gather.9, f32[1,3696,2048]{2,1,0:T(8,128)} %param.15), kind=kOutput, calls=%fused_computation.37 | convolution fusion | flops 968884224 | bytes 31275008 | tf_op jit(solution)/shard_map/dot_general | solution.py:69
  121.9 0.0 reduce-scatter.3.cloned.1.call-update
  121.9 0.0 reduce-scatter.5.cloned.1.call-start
  121.9 0.0 copy-done.2
  121.9 0.1 fusion.14
  122.0 15.1 %all_gather.10 = bf16[64,3696]{1,0:T(8,128)(2,1)S(1)} all-gather(bf16[16,3696]{1,0:T(8,128)(2,1)S(1)} %fusion.14), channel_id=1, replica_groups=mesh['role'=2,'rep'=4,'tp'=4] {'rep'}, dimensions={0}, use_global_device_ids=true | all-gather | bytes 591360 | tf_op jit(solution)/shard_map/all_gather | solution.py:80
  137.1 0.0 copy-done.3
  137.1 0.0 copy-done.4
  137.1 10.8 %reduce-scatter.3.cloned.1.call-done = f32[16,2048]{1,0:T(8,128)} async-done(((f32[64,2048]{1,0:T(8,128)}), f32[16,2048]{1,0:T(8,128)}) %reduce-scatter.3.cloned.1.call-update) | async-done | bytes 131088 | tf_op jit(solution)/shard_map/reduce_scatter | solution.py:68
  147.9 0.0 copy-done.1
  147.9 1.1 convolution_multiply_fusion
  149.0 0.0 collective-permute-done
  149.0 8.9 %fusion.3 = f32[64,2048]{1,0:T(8,128)} fusion(bf16[64,3696]{1,0:T(8,128)(2,1)S(1)} %all_gather.10, bf16[3696,2048]{1,0:T(8,128)(2,1)} %get-tuple-element.12, bf16[3696,2048]{1,0:T(8,128)(2,1)} %collective-permute-done, pred[]{:T(512)S(6)} %eq.16), kind=kOutput, calls=%fused_computation.7 | convolution fusion | flops 976453632 | bytes 31275008 | tf_op jit(solution)/shard_map/dot_general | solution.py:82
  157.9 0.0 reduce-scatter.5.cloned.1.call-update
  157.9 0.0 copy-start
  158.0 27.0 %select_bitcast_fusion = f32[1,3696,2048]{2,1,0:T(8,128)} fusion(f32[3696,2048]{1,0:T(8,128)} %get-tuple-element.13, bf16[3696,2048]{1,0:T(8,128)(2,1)} %collective-permute-done, pred[]{:T(512)S(6)} %eq.16), kind=kLoop, calls=%fused_computation.5 | loop fusion | flops 15138816 | bytes 75694080 | tf_op jit(solution)/shard_map/broadcast_in_dim | solution.py:96
  184.9 0.0 reduce-scatter.5.cloned.1.call-done
  184.9 0.0 copy-done
  184.9 1.6 fusion.19
  (2 shorter events, 0.0 us)
Async XLA Ops:
  7.2 140.7 %reduce-scatter.3.cloned.1.call-start = ((), (), s32[]{:S(2)}) async-start(), calls=%async_computation.2 | async-start | bytes 655360 | tf_op jit(solution)/shard_map/reduce_scatter | solution.py:68
  101.9 20.0 %copy-start.2 = (bf16[1,2,16,3696]{3,2,1,0:T(8,128)(2,1)S(1)}, bf16[1,2,16,3696]{3,2,1,0:T(8,128)(2,1)}, u32[]{:S(2)}) copy-start(bf16[1,2,16,3696]{3,2,1,0:T(8,128)(2,1)} %param.12) | copy-start | bytes 709636
  101.9 35.2 %copy-start.3 = (s32[1,16]{1,0:T(1,128)S(1)}, s32[1,16]{1,0:T(1,128)}, u32[]{:S(2)}) copy-start(s32[1,16]{1,0:T(1,128)} %param.19) | copy-start | bytes 196
  101.9 35.2 %copy-start.4 = (s32[1,16]{1,0:T(1,128)S(1)}, s32[1,16]{1,0:T(1,128)}, u32[]{:S(2)}) copy-start(s32[1,16]{1,0:T(1,128)} %param.18) | copy-start | bytes 196
  101.9 46.0 %copy-start.1 = (bf16[1,2,16,2048]{3,2,1,0:T(8,128)(2,1)S(1)}, bf16[1,2,16,2048]{3,2,1,0:T(8,128)(2,1)}, u32[]{:S(2)}) copy-start(bf16[1,2,16,2048]{3,2,1,0:T(8,128)(2,1)} %param.13) | copy-start | bytes 393220
  101.9 47.1 %collective-permute-start = (bf16[3696,2048]{1,0:T(8,128)(2,1)}, bf16[3696,2048]{1,0:T(8,128)(2,1)}, u32[]{:S(2)}, u32[]{:S(2)}) collective-permute-start(bf16[3696,2048]{1,0:T(8,128)(2,1)} %get-tuple-element.12), channel_id=1, source_target_pairs={{0,16},{1,17},{2,18},{3,19},{4,20},{5,21},{6,22},{7,23},{8,24},{9,... | collective-permute-start | bytes 45416456 | tf_op jit(solution)/shard_map/ppermute | solution.py:21
  121.9 63.1 %reduce-scatter.5.cloned.1.call-start = ((), (), s32[]{:S(2)}) async-start(), calls=%async_computation.3 | async-start | bytes 655360 | tf_op jit(solution)/shard_map/reduce_scatter | solution.py:81
  157.9 27.0 %copy-start = (f32[16,2048]{1,0:T(8,128)S(1)}, f32[16,2048]{1,0:T(8,128)}, u32[]{:S(2)}) copy-start(f32[16,2048]{1,0:T(8,128)} %reduce-scatter.3.cloned.1.call-done) | copy-start | bytes 393220
Sparse Core Ops, SparseCore 0:
  122.0 25.8 reduce-scatter.2
  158.1 25.0 reduce-scatter.4
where the time goes:
time: 194 us; the launch traced here: 193 us
  other arithmetic  84.4 us (44%)
  blocking collectives  41.3 us (21%)
  matrix products  35.9 us (19%)
  between operations  14.1 us (7%)
  waiting for transfers between devices  10.8 us (6%)
  starting transfers between devices  6.85 us (4%)
    convert_element_type x1, other arithmetic, local(): fresh = updated.astype(jnp.bfloat16)  54.7 us
    broadcast_in_dim x2, other arithmetic, local(): return (first_out[None], next_out[None], new_weights[None])  28.6 us
    all_gather x1, blocking collectives, local(): segment = lax.all_gather(hidden, 'rep', axis=0, tiled=True)  16.9 us
    all_gather x1, blocking collectives, local(): piece = lax.all_gather(upcoming, 'rep', axis=0, tiled=True)  15.1 us
    dot_general x1, matrix products, local(): jnp.dot(partial_value, older, preferred_element_type=jnp.float32)  13.1 us
    dot_general x1, matrix products, accumulate(): lax.dot_general(segment, cot_rows, (((0,), (0,)), ((), ())), preferred_el...  12.8 us
    reduce_scatter x1, waiting for transfers between devices, local(): lax.psum_scatter(jnp.dot(partial_value, older, preferred_element_type=jnp...  10.8 us
    all_gather x1, blocking collectives, local(): cot_rows = lax.all_gather(cotangent, 'tp', axis=0, tiled=True)  9.28 us
  transfers between devices with their start and end apart: 3, of which 1 were waited for; matrix products, arithmetic and copies ran while one was open for 21% of the time, Pallas kernels for 0%

commit v1 on v0

v1 whole, which is shorter than its diff:
```python
import functools

import jax
import jax.numpy as jnp
from jax import lax
from jax.experimental import pallas as pl
from jax.experimental.pallas import tpu as pltpu
from jax.sharding import PartitionSpec as P


FF = 14784

beta_one = 0.9
beta_two = 0.95
epsilon = 1e-08
learn_rate = 0.08
decay_rate = 0.1
correct_one = 1.0 - 0.9**60
correct_two = 1.0 - 0.95**60

factor = FF ** (-0.5)
ROOT = (beta_two / correct_two) ** 0.5
GRAD_ONE = (1.0 - beta_one) / beta_one * factor
GRAD_TWO = (1.0 - beta_two) / beta_two * factor * factor
STEP = learn_rate * beta_one / correct_one / ROOT
EPS = epsilon / ROOT
KEEP = 1.0 - learn_rate * decay_rate

TILE = 128
SLOTS = 4
OUT_SLOTS = 4
PIECES = 4
EARLY_TILES = 5
FAR_CHUNKS = 2
STAGE_LIMIT = 22 * 1024 * 1024
EARLY_LIMIT = 2 * 1024 * 1024
WIDE = 256


def activate(both_halves):
    return (
        jax.nn.silu(both_halves[0].astype(jnp.float32)) * both_halves[1].astype(jnp.float32)
    ).astype(jnp.bfloat16)


def tiles_of(low, high):
    return (high - low) // TILE, (high - low) % TILE


def whole_copy(copy, rows):
    source, target, sem = copy
    return pltpu.make_async_copy(source(0, rows), target(0, rows), sem)


def start_pieces(copy, rows):
    source, target, sem = copy
    piece = rows // PIECES if rows % (PIECES * 8) == 0 else rows
    for low in range(0, rows, piece):
        pltpu.make_async_copy(source(low, piece), target(low, piece), sem).start()


def part(ref, base):
    return lambda low, rows: ref.at[pl.ds(pl.multiple_of(base + low, 8), rows)]


def slot_part(ref, slot):
    return lambda low, rows: ref.at[slot, pl.ds(low, rows)]


def run_tiles(low, high, fetch, work, begin=0, before=None):
    full, rest = tiles_of(low, high)

    def start(index, rows):
        for copy in fetch(index, lax.rem(index, SLOTS), rows):
            start_pieces(copy, rows)

    def finish(index, rows):
        for copy in fetch(index, lax.rem(index, SLOTS), rows):
            whole_copy(copy, rows).wait()

    ahead = SLOTS - 1
    for index in range(begin, min(begin + ahead, full)):
        start(jnp.int32(index), TILE)
    if rest and full < begin + ahead:
        start(jnp.int32(full), rest)
    if before is not None:
        before()

    def body(index, carry):
        finish(index, TILE)

        @pl.when(index + ahead < full)
        def _():
            start(index + ahead, TILE)

        if rest and full >= begin + ahead:

            @pl.when(index + ahead == full)
            def _():
                start(jnp.int32(full), rest)

        work(index, lax.rem(index, SLOTS), TILE)
        return carry

    lax.fori_loop(begin, full, body, 0)
    if rest:
        index = jnp.int32(full)
        finish(index, rest)
        work(index, lax.rem(index, SLOTS), rest)


def each_strip(strips, strip):
    for c in range(strips):
        strip(c, 0)


def stage_kernel(plan, *refs):
    learn, first, take = plan["learn"], plan["first"], plan["take"]
    refs = list(refs)
    role, h, nx, cot, w, m1, m2 = refs[:7]
    refs = refs[7:]
    if plan["carry"]:
        acc_one_in, acc_two_in = refs[0], refs[1]
        refs = refs[3:]
    got = refs.pop(0) if take else None
    early = [refs.pop(0) for _ in range(3)] if plan["early"] else None
    past = refs.pop(0) if plan["past"] else None
    acc_one, acc_two, upd = refs[:3]
    refs = refs[3:]
    fresh = refs.pop(0) if learn else None
    w_buf, m1_buf, m2_buf, u_buf, b_buf, in_sem, out_sem, b_sem = refs
    width = cot.shape[1]
    wide = min(WIDE, width)
    strips = width // wide

    if plan["carry"]:
        acc_one[...] = acc_one_in[...]
        acc_two[...] = acc_two_in[...]
    else:
        acc_one[...] = jnp.zeros_like(acc_one)
        acc_two[...] = jnp.zeros_like(acc_two)

    def out_copy(base, index):
        slot = lax.rem(index, OUT_SLOTS)
        return slot_part(u_buf, slot), part(upd, base + index * TILE), out_sem.at[slot]

    def fresh_copy(index):
        slot = lax.rem(index, OUT_SLOTS)
        return slot_part(b_buf, slot), part(fresh, index * TILE), b_sem.at[slot]

    def drain(copy_of, low, high):
        full, rest = tiles_of(low, high)
        sizes = [TILE] * full + ([rest] if rest else [])
        for index in range(max(0, len(sizes) - OUT_SLOTS), len(sizes)):
            whole_copy(copy_of(jnp.int32(index)), sizes[index]).wait()

    def learner():
        low, high = learn

        def fetch(index, slot, rows):
            return [
                (part(src, low + index * TILE), slot_part(dst, slot), in_sem.at[slot, k])
                for k, (src, dst) in enumerate(((w, w_buf), (m1, m1_buf), (m2, m2_buf)))
            ]

        def work(index, slot, rows, held=None):
            outgoing = lax.rem(index, OUT_SLOTS)

            @pl.when(index >= OUT_SLOTS)
            def _():
                whole_copy(out_copy(low, index - OUT_SLOTS), TILE).wait()
                if plan["far"]:
                    whole_copy(fresh_copy(index - OUT_SLOTS), TILE).wait()

            lanes = pl.ds(pl.multiple_of(low + index * TILE, TILE), rows)
            here = pl.ds(0, rows)
            hb = h[:, lanes]
            nb = nx[:, lanes] if plan["second"] else None
            local_rows = pl.ds(pl.multiple_of(index * TILE, TILE), rows)

            def read(which, cols):
                if held is not None:
                    return early[which][local_rows, cols]
                return (w_buf, m1_buf, m2_buf)[which][slot, here, cols]

            def strip(c, carry):
                cols = pl.ds(c * wide, wide)
                wv = read(0, cols)
                acc_one[:, cols] += jnp.dot(
                    hb, wv.astype(jnp.bfloat16), preferred_element_type=jnp.float32
                )
                grad = lax.dot_general(
                    hb, cot[:, cols], (((0,), (0,)), ((), ())), preferred_element_type=jnp.float32
                )
                top = read(1, cols) + GRAD_ONE * grad
                square = read(2, cols) + GRAD_TWO * (grad * grad)
                low_part = square * lax.rsqrt(square) + EPS
                updated = KEEP * wv - STEP * (top / low_part)
                u_buf[outgoing, here, cols] = updated
                fb = updated.astype(jnp.bfloat16)
                if plan["far"]:
                    b_buf[outgoing, here, cols] = fb
                else:
                    fresh[local_rows, cols] = fb
                if plan["second"]:
                    acc_two[:, cols] += jnp.dot(nb, fb, preferred_element_type=jnp.float32)

            each_strip(strips, strip)
            start_pieces(out_copy(low, index), rows)
            if plan["far"]:
                start_pieces(fresh_copy(index), rows)

        def first_tiles():
            def body(index, carry):
                work(index, None, TILE, held=True)
                return carry

            if plan["early"]:
                lax.fori_loop(0, plan["early"], body, 0)
            if plan["past"]:
                second_of_past()

        run_tiles(low, high, fetch, work, plan["early"], first_tiles)
        drain(lambda index: out_copy(low, index), low, high)
        if plan["far"]:
            drain(fresh_copy, low, high)

    def second_of_past():
        start, stop = plan["past"]
        full, rest = tiles_of(start, stop)

        def work(index, rows):
            nb = nx[:, pl.ds(pl.multiple_of(start + index * TILE, TILE), rows)]

            def strip(c, carry):
                cols = pl.ds(c * wide, wide)
                fb = past[pl.ds(pl.multiple_of(index * TILE, TILE), rows), cols]
                acc_two[:, cols] += jnp.dot(nb, fb, preferred_element_type=jnp.float32)

            each_strip(strips, strip)

        def body(index, carry):
            work(index, TILE)
            return carry

        lax.fori_loop(0, full, body, 0)
        if rest:
            work(jnp.int32(full), rest)

    def rollout_first():
        low, high = first

        def fetch(index, slot, rows):
            return [(part(w, low + index * TILE), slot_part(w_buf, slot), in_sem.at[slot, 0])]

        def work(index, slot, rows):
            hb = h[:, pl.ds(pl.multiple_of(low + index * TILE, TILE), rows)]

            def strip(c, carry):
                cols = pl.ds(c * wide, wide)
                acc_one[:, cols] += jnp.dot(
                    hb,
                    w_buf[slot, pl.ds(0, rows), cols].astype(jnp.bfloat16),
                    preferred_element_type=jnp.float32,
                )
                return carry

            each_strip(strips, strip)

        run_tiles(low, high, fetch, work)

    def rollout_take():
        low, high = take
        full, rest = tiles_of(low, high)

        def work(index, slot, rows):
            outgoing = lax.rem(index, OUT_SLOTS)

            @pl.when(index >= OUT_SLOTS)
            def _():
                whole_copy(out_copy(low, index - OUT_SLOTS), TILE).wait()

            nb = nx[:, pl.ds(pl.multiple_of(low + index * TILE, TILE), rows)]

            def strip(c, carry):
                cols = pl.ds(c * wide, wide)
                if plan["take_far"]:
                    fb = b_buf[slot, pl.ds(0, rows), cols]
                else:
                    fb = got[pl.ds(pl.multiple_of(index * TILE, TILE), rows), cols]
                u_buf[outgoing, pl.ds(0, rows), cols] = fb.astype(jnp.float32)
                acc_two[:, cols] += jnp.dot(nb, fb, preferred_element_type=jnp.float32)

            each_strip(strips, strip)
            start_pieces(out_copy(low, index), rows)

        if plan["take_far"]:

            def fetch(index, slot, rows):
                return [(part(got, index * TILE), slot_part(b_buf, slot), in_sem.at[slot, 0])]

            run_tiles(low, high, fetch, work)
        else:

            def body(index, carry):
                work(index, None, TILE)
                return carry

            lax.fori_loop(0, full, body, 0)
            if rest:
                work(jnp.int32(full), None, rest)
        drain(lambda index: out_copy(low, index), low, high)

    if learn:
        pl.when(role[0] == 0)(learner)
    if first:
        pl.when(role[0] == 1)(rollout_first)
    if take:
        pl.when(role[0] == 1)(rollout_take)


def early_kernel(w, m1, m2, w_out, m1_out, m2_out, sems):
    rows = w_out.shape[0]
    copies = [
        (part(src, 0), part(dst, 0), sems.at[k])
        for k, (src, dst) in enumerate(((w, w_out), (m1, m1_out), (m2, m2_out)))
    ]
    for low in range(0, rows, TILE):
        for source, target, sem in copies:
            pltpu.make_async_copy(source(low, TILE), target(low, TILE), sem).start()
    for copy in copies:
        whole_copy(copy, rows).wait()


def fetch_early(tiles, w, m1, m2):
    shape = pltpu.VMEM((tiles * TILE, w.shape[1]), jnp.float32)
    size = 12 * tiles * TILE * w.shape[1]
    return pl.pallas_call(
        early_kernel,
        out_shape=[shape] * 3,
        in_specs=[pl.BlockSpec(memory_space=pl.ANY)] * 3,
        out_specs=[pl.BlockSpec(memory_space=pltpu.VMEM)] * 3,
        scratch_shapes=[pltpu.SemaphoreType.DMA((3,))],
        compiler_params=pltpu.CompilerParams(vmem_limit_bytes=EARLY_LIMIT),
        cost_estimate=pl.CostEstimate(flops=size * 16, bytes_accessed=2 * size, transcendentals=0),
    )(w, m1, m2)


def stage(plan, role, h, nx, cot, w, m1, m2, state, got, early, past):
    rows, width = h.shape[0], cot.shape[1]
    height = w.shape[0]
    vmem = pl.BlockSpec(memory_space=pltpu.VMEM)
    hbm = pl.BlockSpec(memory_space=pl.ANY)
    args = [role, h, nx, cot, w, m1, m2]
    specs = [pl.BlockSpec(memory_space=pltpu.SMEM)] + [vmem] * 3 + [hbm] * 3
    alias = {}
    if state is not None:
        args += list(state)
        specs += [vmem, vmem, hbm]
        alias = {9: 2}
    if plan["take"]:
        if plan["take_far"]:
            got = pltpu.with_memory_space_constraint(got, pltpu.HBM)
        args.append(got)
        specs.append(hbm if plan["take_far"] else vmem)
    if early is not None:
        args += early
        specs += [vmem] * 3
    if past is not None:
        args.append(past)
        specs.append(vmem)
    out = [
        jax.ShapeDtypeStruct((rows, width), jnp.float32),
        jax.ShapeDtypeStruct((rows, width), jnp.float32),
        jax.ShapeDtypeStruct((height, width), jnp.float32),
    ]
    out_specs = [vmem, vmem, hbm]
    span = 0
    if plan["learn"]:
        span = plan["learn"][1] - plan["learn"][0]
        where = pltpu.HBM if plan["far"] else pltpu.VMEM
        out.append(where((span, width), jnp.bfloat16))
        out_specs.append(hbm if plan["far"] else vmem)
    plan = dict(
        plan,
        carry=state is not None,
        early=early[0].shape[0] // TILE if early is not None else 0,
    )
    cost = pl.CostEstimate(
        flops=int(3e6 + 6 * rows * width * max(span, 64)),
        bytes_accessed=int(20 * span * width + 1e6),
        transcendentals=0,
    )
    return pl.pallas_call(
        functools.partial(stage_kernel, plan),
        out_shape=out,
        in_specs=specs,
        out_specs=out_specs,
        scratch_shapes=[
            pltpu.VMEM((SLOTS, TILE, width), jnp.float32),
            pltpu.VMEM((SLOTS, TILE, width), jnp.float32),
            pltpu.VMEM((SLOTS, TILE, width), jnp.float32),
            pltpu.VMEM((OUT_SLOTS, TILE, width), jnp.float32),
            pltpu.VMEM((OUT_SLOTS, TILE, width), jnp.bfloat16),
            pltpu.SemaphoreType.DMA((SLOTS, 3)),
            pltpu.SemaphoreType.DMA((OUT_SLOTS,)),
            pltpu.SemaphoreType.DMA((OUT_SLOTS,)),
        ],
        input_output_aliases=alias,
        compiler_params=pltpu.CompilerParams(vmem_limit_bytes=STAGE_LIMIT),
        cost_estimate=cost,
    )(*args)


def shifts_of(piece, axis):
    size = lax.axis_size(axis)
    came = []
    for by in range(1, size):
        came.append(lax.ppermute(piece, axis, [(i, (i + by) % size) for i in range(size)]))
    return came


def in_order(pieces, axis):
    size = lax.axis_size(axis)
    me = lax.axis_index(axis)
    rows, width = pieces[0].shape
    whole = jnp.zeros((rows * size, width), pieces[0].dtype)
    for by, piece in enumerate(pieces):
        whole = lax.dynamic_update_slice_in_dim(whole, piece, ((me - by) % size) * rows, 0)
    return whole


def scatter_sum(partials, axis):
    size = lax.axis_size(axis)
    if size > 4 or size & (size - 1):
        return lax.psum_scatter(partials, axis, scatter_dimension=1, tiled=True)
    rows = partials.shape[1] // size
    me = lax.axis_index(axis)
    total = lax.dynamic_slice_in_dim(partials, me * rows, rows, 1)
    sent = partials.astype(jnp.bfloat16)
    for mask in range(1, size):
        piece = lax.dynamic_slice_in_dim(sent, (me ^ mask) * rows, rows, 1)
        came = lax.ppermute(piece, axis, [(i, i ^ mask) for i in range(size)])
        total = total + came.astype(jnp.float32)
    return total


SHARES = (0.36, 0.31, 0.21, 0.12)


def cut(height):
    tiles = -(-height // TILE)
    marks = [0]
    done = 0.0
    for share in SHARES[:-1]:
        done += share
        marks.append(max(marks[-1] + 1, min(tiles, round(done * tiles))))
    marks.append(tiles)
    return [(a * TILE, min(b * TILE, height)) for a, b in zip(marks, marks[1:])]


def compute(
    pre_act,
    next_pre,
    stream,
    cotangent,
    weights,
    first_moment,
    second_moment,
    tree_parent,
    tree_depth,
):
    role = lax.axis_index("role").astype(jnp.int32).reshape(1)
    w, first_moment, second_moment = [
        pltpu.with_memory_space_constraint(array, pltpu.HBM)
        for array in (weights[0], first_moment, second_moment)
    ]
    height = w.shape[0]
    chunks = cut(height)
    count = len(chunks)

    hidden = activate(pre_act[0])
    upcoming = activate(next_pre[0])
    early = None
    if lax.axis_size("rep") > 8:
        h = lax.all_gather(hidden, "rep", axis=0, tiled=True)
        nx = lax.all_gather(upcoming, "rep", axis=0, tiled=True)
        cot_rows = lax.all_gather(cotangent, "tp", axis=0, tiled=True)
    else:
        came = shifts_of(hidden, "rep")
        cot_came = shifts_of(cotangent, "tp")
        tiles = min(EARLY_TILES, tiles_of(*chunks[0])[0])
        if tiles:
            early = fetch_early(tiles, w, first_moment, second_moment)
        h = in_order([hidden] + came, "rep")
        cot_rows = in_order([cotangent] + cot_came, "tp")
        upcoming, _ = lax.optimization_barrier((upcoming, came))
        nx = in_order([upcoming] + shifts_of(upcoming, "rep"), "rep")

    state = None
    made, flying = [], []
    for step in range(count + 2):
        far = step >= count - FAR_CHUNKS
        plan = {
            "learn": chunks[step] if step < count else None,
            "first": (0, height) if step == 0 else None,
            "take": chunks[step - 2] if step >= 2 else None,
            "second": step > 0,
            "past": chunks[0] if step == 1 else None,
            "far": far,
            "take_far": step - 2 >= count - FAR_CHUNKS,
        }
        result = stage(
            plan,
            role,
            h,
            h if step == 0 else nx,
            cot_rows,
            w,
            first_moment,
            second_moment,
            state,
            flying[step - 2] if step >= 2 else None,
            early if step == 0 else None,
            made[0] if step == 1 else None,
        )
        state = tuple(result[:3])
        if step < count:
            made.append(result[3])
            flying.append(lax.ppermute(result[3], "role", [(0, 1), (1, 0)]))
    sums = scatter_sum(jnp.stack(state[:2]), "tp")
    first_sum, next_sum = sums[0], sums[1]
    new_weights = state[2]

    first_out = (stream[0, 0].astype(jnp.float32) + factor * first_sum).astype(jnp.bfloat16)
    block_rows = first_out.shape[0]
    local_parent = tree_parent[0] - lax.axis_index("tp") * block_rows
    onehot = (local_parent[:, None] == jnp.arange(block_rows, dtype=jnp.int32)[None, :]).astype(
        jnp.bfloat16
    )
    picked = jnp.dot(onehot, first_out, preferred_element_type=jnp.float32)
    portion = 1.0 / (1.0 + tree_depth[0].astype(jnp.float32))
    total = stream[0, 1].astype(jnp.float32) + factor * next_sum + picked * portion[:, None]
    next_out = total.astype(jnp.bfloat16)
    return (first_out[None], next_out[None], new_weights[None])


def solution(mesh):
    placed = (
        P("role", None, "rep", "tp"),
        P("role", None, "rep", "tp"),
        P("role", None, "tp", "rep"),
        P("tp", "rep"),
        P("role", "tp", "rep"),
        P("tp", "rep"),
        P("tp", "rep"),
        P("role", "tp"),
        P("role", "tp"),
    )
    return jax.shard_map(
        compute,
        mesh=mesh,
        in_specs=placed,
        out_specs=(P("role", "tp", "rep"), P("role", "tp", "rep"), P("role", "tp", "rep")),
        check_vma=False,
    )
```

time: 194 us -> 97.1 us (0.50)
  the two profiles are of different devices: /device:TPU:0 before, /device:TPU:9 now
where the time goes in v1:
time: 97.1 us; the launch traced here: 96.6 us
  starting transfers between devices  39.2 us (40%)
  Pallas kernels  36 us (37%)
  waiting for transfers between devices  16.6 us (17%)
  other arithmetic  1.91 us (2%)
  local copies, waits for them, and re-layouts  1.17 us (1%)
    pallas_call x6, Pallas kernels, stage(): pl.pallas_call(functools.partial(stage_kernel, plan), out_shape=out, in_s...  30.5 us
    ppermute x4, starting transfers between devices, compute(): flying.append(lax.ppermute(result[3], 'role', [(0, 1), (1, 0)]))  25.8 us
    ppermute x9, waiting for transfers between devices, shifts_of(): lax.ppermute(piece, axis, [(i, (i + by) % size) for i in range(size)])  12.2 us
    ppermute x9, starting transfers between devices, shifts_of(): lax.ppermute(piece, axis, [(i, (i + by) % size) for i in range(size)])  10.7 us
    pallas_call x1, Pallas kernels, fetch_early(): pl.pallas_call(early_kernel, out_shape=[shape] * 3, in_specs=[pl.BlockSpe...  5.54 us
    ppermute x3, waiting for transfers between devices, scatter_sum(): came = lax.ppermute(piece, axis, [(i, i ^ mask) for i in range(size)])  4.4 us
    ppermute x3, starting transfers between devices, scatter_sum(): came = lax.ppermute(piece, axis, [(i, i ^ mask) for i in range(size)])  2.71 us
  transfers between devices with their start and end apart: 16, of which 7 were waited for; matrix products, arithmetic and copies ran while one was open for 1% of the time, Pallas kernels for 20%

profile of v1, /device:TPU:9, one launch (start us, length us, event | category | flops | bytes accessed | tf_op | source)
XLA Modules:
  0.0 96.6 jit_solution(11613414290184822657)
XLA Ops:
  0.7 1.1 %constant_dynamic-update-slice_fusion.11 = (bf16[64,3696]{1,0:T(8,128)(2,1)S(1)}, bf16[16,3696]{1,0:T(8,128)(2,1)S(1)}) fusion(bf16[64,3696]{1,0:T(8,128)(2,1)S(1)} %broadcast.42.clone, s32[]{:T(128)S(6)} %select_n.84, bf16[1,2,16,3696]{3,2,1,0:T(8,128)(2,1)} %param.9), kind=kLoop, calls=%fused_computation.53 | loop fusion | flops 473088 | bytes 474116 | tf_op jit(solution)/shard_map/dynamic_update_slice | solution.py:429
  1.7 1.3 %collective-permute-start = (bf16[16,3696]{1,0:T(8,128)(2,1)S(1)}, bf16[16,3696]{1,0:T(8,128)(2,1)S(1)}, u32[]{:S(2)}, u32[]{:S(2)}) collective-permute-start(bf16[16,3696]{1,0:T(8,128)(2,1)S(1)} %get-tuple-element.56), channel_id=1, source_target_pairs={{0,4},{4,8},{8,12},{12,0},{1,5},{5,9},{9,13},{13,1},{2,6},{6,10},{... | collective-permute-start | bytes 354824 | tf_op jit(solution)/shard_map/ppermute | solution.py:419
  3.1 1.1 %collective-permute-start.1 = (bf16[16,3696]{1,0:T(8,128)(2,1)S(1)}, bf16[16,3696]{1,0:T(8,128)(2,1)S(1)}, u32[]{:S(2)}, u32[]{:S(2)}) collective-permute-start(bf16[16,3696]{1,0:T(8,128)(2,1)S(1)} %get-tuple-element.56), channel_id=1, source_target_pairs={{0,8},{4,12},{8,0},{12,4},{1,9},{5,13},{9,1},{13,5},{2,10},{6,14},... | collective-permute-start | bytes 354824 | tf_op jit(solution)/shard_map/ppermute | solution.py:419
  4.2 1.4 %collective-permute-start.2 = (bf16[16,3696]{1,0:T(8,128)(2,1)S(1)}, bf16[16,3696]{1,0:T(8,128)(2,1)S(1)}, u32[]{:S(2)}, u32[]{:S(2)}) collective-permute-start(bf16[16,3696]{1,0:T(8,128)(2,1)S(1)} %get-tuple-element.56), channel_id=1, source_target_pairs={{0,12},{4,0},{8,4},{12,8},{1,13},{5,1},{9,5},{13,9},{2,14},{6,2},{... | collective-permute-start | bytes 354824 | tf_op jit(solution)/shard_map/ppermute | solution.py:419
  5.6 1.2 %collective-permute-start.6 = (bf16[16,2048]{1,0:T(8,128)(2,1)}, bf16[16,2048]{1,0:T(8,128)(2,1)S(1)}, u32[]{:S(2)}, u32[]{:S(2)}) collective-permute-start(bf16[16,2048]{1,0:T(8,128)(2,1)} %param.12), channel_id=1, source_target_pairs={{0,1},{1,2},{2,3},{3,0},{4,5},{5,6},{6,7},{7,4},{8,9},{9,10},{10,1... | collective-permute-start | bytes 196616 | tf_op jit(solution)/shard_map/ppermute | solution.py:419
  6.8 1.2 %collective-permute-start.7 = (bf16[16,2048]{1,0:T(8,128)(2,1)}, bf16[16,2048]{1,0:T(8,128)(2,1)S(1)}, u32[]{:S(2)}, u32[]{:S(2)}) collective-permute-start(bf16[16,2048]{1,0:T(8,128)(2,1)} %param.12), channel_id=1, source_target_pairs={{0,2},{1,3},{2,0},{3,1},{4,6},{5,7},{6,4},{7,5},{8,10},{9,11},{10,... | collective-permute-start | bytes 196616 | tf_op jit(solution)/shard_map/ppermute | solution.py:419
  8.0 0.9 constant_dynamic-update-slice_fusion.3
  8.9 0.0 copy-start.1
  8.9 5.5 %shard_map.112 = (f32[640,2048]{1,0:T(8,128)S(1)}, f32[640,2048]{1,0:T(8,128)S(1)}, f32[640,2048]{1,0:T(8,128)S(1)}) custom-call(f32[3696,2048]{1,0:T(8,128)} %bitcast.54, f32[3696,2048]{1,0:T(8,128)} %refs_5_.11, f32[3696,2048]{1,0:T(8,128)} %refs_6_.11), custom_call_target="tpu_custom_call" | custom-call | flops 251658240 | bytes 31457280 | tf_op jit(solution)/shard_map/pallas_call | solution.py:338
  14.5 0.0 collective-permute-done.6
  14.5 0.0 copy-done.1
  14.5 1.2 %collective-permute-start.8 = (bf16[16,2048]{1,0:T(8,128)(2,1)S(1)}, bf16[16,2048]{1,0:T(8,128)(2,1)S(1)}, u32[]{:S(2)}, u32[]{:S(2)}) collective-permute-start(bf16[16,2048]{1,0:T(8,128)(2,1)S(1)} %copy-done.1), channel_id=1, source_target_pairs={{0,3},{1,0},{2,1},{3,2},{4,7},{5,4},{6,5},{7,6},{8,11},{9,8},{10,9... | collective-permute-start | bytes 196616 | tf_op jit(solution)/shard_map/ppermute | solution.py:419
  15.7 0.0 collective-permute-done.7
  15.7 1.9 %collective-permute-done.8 = bf16[16,2048]{1,0:T(8,128)(2,1)S(1)} collective-permute-done((bf16[16,2048]{1,0:T(8,128)(2,1)S(1)}, bf16[16,2048]{1,0:T(8,128)(2,1)S(1)}, u32[]{:S(2)}, u32[]{:S(2)}) %collective-permute-start.8) | collective-permute-done | bytes 65568 | tf_op jit(solution)/shard_map/ppermute | solution.py:419
  17.7 0.0 collective-permute-done
  17.7 0.0 collective-permute-done.1
  17.7 0.0 collective-permute-done.2
  17.8 0.0 copy-start
  17.8 14.0 %shard_map.113 = (f32[64,2048]{1,0:T(8,128)S(1)}, f32[64,2048]{1,0:T(8,128)S(1)}, f32[3696,2048]{1,0:T(8,128)}, bf16[1280,2048]{1,0:T(8,128)(2,1)S(1)}) custom-call(s32[1]{0:T(128)} %bitcast.1.refs_0_, bf16[64,3696]{1,0:T(8,128)(2,1)S(1)} %constant_dynamic-update-slice_fusion.8.refs_1_.refs_2_, ...), custom_call_target="tpu_custom_call" | custom-call | flops 1009632960 | bytes 53428800 | tf_op jit(solution)/shard_map/pallas_call | solution.py:394
  31.7 0.1 collective-permute-start.9
  31.8 0.0 copy-done
  31.8 0.1 fusion.16
  31.9 0.1 collective-permute-start.3
  32.0 3.1 %collective-permute-start.4 = (bf16[16,3696]{1,0:T(8,128)(2,1)S(1)}, bf16[16,3696]{1,0:T(8,128)(2,1)S(1)}, u32[]{:S(2)}, u32[]{:S(2)}) collective-permute-start(bf16[16,3696]{1,0:T(8,128)(2,1)S(1)} %fusion.16), channel_id=1, source_target_pairs={{0,8},{4,12},{8,0},{12,4},{1,9},{5,13},{9,1},{13,5},{2,10},{6,14},... | collective-permute-start | bytes 354824 | tf_op jit(solution)/shard_map/ppermute | solution.py:419
  35.1 0.0 collective-permute-start.5
  35.2 1.1 %collective-permute-done.3 = bf16[16,3696]{1,0:T(8,128)(2,1)S(1)} collective-permute-done((bf16[16,3696]{1,0:T(8,128)(2,1)S(1)}, bf16[16,3696]{1,0:T(8,128)(2,1)S(1)}, u32[]{:S(2)}, u32[]{:S(2)}) %collective-permute-start.3) | collective-permute-done | bytes 118304 | tf_op jit(solution)/shard_map/ppermute | solution.py:419
  36.3 6.2 %collective-permute-done.4 = bf16[16,3696]{1,0:T(8,128)(2,1)S(1)} collective-permute-done((bf16[16,3696]{1,0:T(8,128)(2,1)S(1)}, bf16[16,3696]{1,0:T(8,128)(2,1)S(1)}, u32[]{:S(2)}, u32[]{:S(2)}) %collective-permute-start.4) | collective-permute-done | bytes 118304 | tf_op jit(solution)/shard_map/ppermute | solution.py:419
  42.5 3.0 %collective-permute-done.5 = bf16[16,3696]{1,0:T(8,128)(2,1)S(1)} collective-permute-done((bf16[16,3696]{1,0:T(8,128)(2,1)S(1)}, bf16[16,3696]{1,0:T(8,128)(2,1)S(1)}, u32[]{:S(2)}, u32[]{:S(2)}) %collective-permute-start.5) | collective-permute-done | bytes 118304 | tf_op jit(solution)/shard_map/ppermute | solution.py:419
  45.5 0.3 shard_map.114
  45.7 14.7 %collective-permute-start.10 = (bf16[1152,2048]{1,0:T(8,128)(2,1)S(1)}, bf16[1152,2048]{1,0:T(8,128)(2,1)S(1)}, u32[]{:S(2)}, u32[]{:S(2)}) collective-permute-start(bf16[1152,2048]{1,0:T(8,128)(2,1)S(1)} %get-tuple-element.43), channel_id=1, source_target_pairs={{0,16},{16,0},{1,17},{17,1},{2,18},{18,2},{3,19},{19,3},{4,20},{20... | collective-permute-start | bytes 14155784 | tf_op jit(solution)/shard_map/ppermute | solution.py:530
  60.4 0.0 collective-permute-done.9.refs_10_
  60.4 4.2 %shard_map.115 = (f32[64,2048]{1,0:T(8,128)S(1)}, f32[64,2048]{1,0:T(8,128)S(1)}, f32[3696,2048]{1,0:T(8,128)}, bf16[896,2048]{1,0:T(8,128)(2,1)}) custom-call(s32[1]{0:T(128)} %bitcast.1.refs_0_, bf16[64,3696]{1,0:T(8,128)(2,1)S(1)} %constant_dynamic-update-slice_fusion.8.refs_1_.refs_2_, ...), custom_call_target="tpu_custom_call", output_to_operand_aliasing={{2}: (9, {})} | custom-call | flops 707643072 | bytes 37700160 | tf_op jit(solution)/shard_map/pallas_call | solution.py:394
  64.7 8.2 %collective-permute-start.11 = (bf16[896,2048]{1,0:T(8,128)(2,1)}, bf16[896,2048]{1,0:T(8,128)(2,1)}, u32[]{:S(2)}, u32[]{:S(2)}) collective-permute-start(bf16[896,2048]{1,0:T(8,128)(2,1)} %get-tuple-element.47), channel_id=1, source_target_pairs={{0,16},{16,0},{1,17},{17,1},{2,18},{18,2},{3,19},{19,3},{4,20},{20... | collective-permute-start | bytes 11010056 | tf_op jit(solution)/shard_map/ppermute | solution.py:530
  72.9 0.0 collective-permute-done.10.refs_10_
  72.9 0.0 copy-start.3
  72.9 3.9 %shard_map.116 = (f32[64,2048]{1,0:T(8,128)S(1)}, f32[64,2048]{1,0:T(8,128)S(1)}, f32[3696,2048]{1,0:T(8,128)}, bf16[368,2048]{1,0:T(8,128)(2,1)}) custom-call(s32[1]{0:T(128)} %bitcast.1.refs_0_, bf16[64,3696]{1,0:T(8,128)(2,1)S(1)} %constant_dynamic-update-slice_fusion.8.refs_1_.refs_2_, ...), custom_call_target="tpu_custom_call", output_to_operand_aliasing={{2}: (9, {})} | custom-call | flops 292406976 | bytes 16073280 | tf_op jit(solution)/shard_map/pallas_call | solution.py:394
  76.8 2.8 %collective-permute-start.12 = (bf16[368,2048]{1,0:T(8,128)(2,1)}, bf16[368,2048]{1,0:T(8,128)(2,1)}, u32[]{:S(2)}, u32[]{:S(2)}) collective-permute-start(bf16[368,2048]{1,0:T(8,128)(2,1)} %get-tuple-element.51), channel_id=1, source_target_pairs={{0,16},{16,0},{1,17},{17,1},{2,18},{18,2},{3,19},{19,3},{4,20},{20... | collective-permute-start | bytes 4521992 | tf_op jit(solution)/shard_map/ppermute | solution.py:530
  79.6 0.0 copy-done.3
  79.6 0.0 collective-permute-done.11.refs_10_
  79.7 5.1 %shard_map.117 = (f32[64,2048]{1,0:T(8,128)S(1)}, f32[64,2048]{1,0:T(8,128)S(1)}, f32[3696,2048]{1,0:T(8,128)}) custom-call(s32[1]{0:T(128)} %bitcast.1.refs_0_, bf16[64,3696]{1,0:T(8,128)(2,1)S(1)} %constant_dynamic-update-slice_fusion.8.refs_1_.refs_2_, ...), custom_call_target="tpu_custom_call", output_to_operand_aliasing={{2}: (9, {})} | custom-call | flops 53331648 | bytes 1000000 | tf_op jit(solution)/shard_map/pallas_call | solution.py:394
  84.8 0.0 collective-permute-done.12.refs_10_
  84.8 0.0 copy-start.4
  84.8 0.0 copy-start.2
  84.8 3.0 %shard_map.118 = (f32[64,2048]{1,0:T(8,128)S(1)}, f32[64,2048]{1,0:T(8,128)S(1)}, f32[3696,2048]{1,0:T(8,128)}) custom-call(s32[1]{0:T(128)} %bitcast.1.refs_0_, bf16[64,3696]{1,0:T(8,128)(2,1)S(1)} %constant_dynamic-update-slice_fusion.8.refs_1_.refs_2_, ...), custom_call_target="tpu_custom_call", output_to_operand_aliasing={{2}: (9, {})} | custom-call | flops 53331648 | bytes 1000000 | tf_op jit(solution)/shard_map/pallas_call | solution.py:394
  87.8 0.1 fusion.3
  88.0 1.2 %collective-permute-start.13 = (bf16[2,16,2048]{2,1,0:T(8,128)(2,1)S(1)}, bf16[2,16,2048]{2,1,0:T(8,128)(2,1)S(1)}, u32[]{:S(2)}, u32[]{:S(2)}) collective-permute-start(bf16[2,16,2048]{2,1,0:T(8,128)(2,1)S(1)} %get-tuple-element.57), channel_id=1, source_target_pairs={{0,1},{1,0},{2,3},{3,2},{4,5},{5,4},{6,7},{7,6},{8,9},{9,8},{10,11... | collective-permute-start | bytes 393224 | tf_op jit(solution)/shard_map/ppermute | solution.py:443
  89.1 1.2 %collective-permute-start.14 = (bf16[2,16,2048]{2,1,0:T(8,128)(2,1)S(1)}, bf16[2,16,2048]{2,1,0:T(8,128)(2,1)S(1)}, u32[]{:S(2)}, u32[]{:S(2)}) collective-permute-start(bf16[2,16,2048]{2,1,0:T(8,128)(2,1)S(1)} %get-tuple-element.59), channel_id=1, source_target_pairs={{0,2},{1,3},{2,0},{3,1},{4,6},{5,7},{6,4},{7,5},{8,10},{9,11},{10,... | collective-permute-start | bytes 393224 | tf_op jit(solution)/shard_map/ppermute | solution.py:443
  90.4 0.3 collective-permute-start.15
  90.7 0.0 copy-done.4
  90.7 1.9 %collective-permute-done.13 = bf16[2,16,2048]{2,1,0:T(8,128)(2,1)S(1)} collective-permute-done((bf16[2,16,2048]{2,1,0:T(8,128)(2,1)S(1)}, bf16[2,16,2048]{2,1,0:T(8,128)(2,1)S(1)}, u32[]{:S(2)}, u32[]{:S(2)}) %collective-permute-start.13) | collective-permute-done | bytes 131104 | tf_op jit(solution)/shard_map/ppermute | solution.py:443
  92.6 0.9 collective-permute-done.14
  93.5 1.6 %collective-permute-done.15 = bf16[2,16,2048]{2,1,0:T(8,128)(2,1)S(1)} collective-permute-done((bf16[2,16,2048]{2,1,0:T(8,128)(2,1)S(1)}, bf16[2,16,2048]{2,1,0:T(8,128)(2,1)S(1)}, u32[]{:S(2)}, u32[]{:S(2)}) %collective-permute-start.15) | collective-permute-done | bytes 131104 | tf_op jit(solution)/shard_map/ppermute | solution.py:443
  95.1 0.1 fusion.7
  95.1 0.0 copy-done.2
  95.2 0.6 fusion.19
  95.8 0.8 fusion.2
  (16 shorter events, 0.3 us)
Async XLA Ops:
  1.7 15.9 %collective-permute-start = (bf16[16,3696]{1,0:T(8,128)(2,1)S(1)}, bf16[16,3696]{1,0:T(8,128)(2,1)S(1)}, u32[]{:S(2)}, u32[]{:S(2)}) collective-permute-start(bf16[16,3696]{1,0:T(8,128)(2,1)S(1)} %get-tuple-element.56), channel_id=1, source_target_pairs={{0,4},{4,8},{8,12},{12,0},{1,5},{5,9},{9,13},{13,1},{2,6},{6,10},{... | collective-permute-start | bytes 354824 | tf_op jit(solution)/shard_map/ppermute | solution.py:419
  3.1 14.6 %collective-permute-start.1 = (bf16[16,3696]{1,0:T(8,128)(2,1)S(1)}, bf16[16,3696]{1,0:T(8,128)(2,1)S(1)}, u32[]{:S(2)}, u32[]{:S(2)}) collective-permute-start(bf16[16,3696]{1,0:T(8,128)(2,1)S(1)} %get-tuple-element.56), channel_id=1, source_target_pairs={{0,8},{4,12},{8,0},{12,4},{1,9},{5,13},{9,1},{13,5},{2,10},{6,14},... | collective-permute-start | bytes 354824 | tf_op jit(solution)/shard_map/ppermute | solution.py:419
  4.2 13.5 %collective-permute-start.2 = (bf16[16,3696]{1,0:T(8,128)(2,1)S(1)}, bf16[16,3696]{1,0:T(8,128)(2,1)S(1)}, u32[]{:S(2)}, u32[]{:S(2)}) collective-permute-start(bf16[16,3696]{1,0:T(8,128)(2,1)S(1)} %get-tuple-element.56), channel_id=1, source_target_pairs={{0,12},{4,0},{8,4},{12,8},{1,13},{5,1},{9,5},{13,9},{2,14},{6,2},{... | collective-permute-start | bytes 354824 | tf_op jit(solution)/shard_map/ppermute | solution.py:419
  5.6 8.9 %collective-permute-start.6 = (bf16[16,2048]{1,0:T(8,128)(2,1)}, bf16[16,2048]{1,0:T(8,128)(2,1)S(1)}, u32[]{:S(2)}, u32[]{:S(2)}) collective-permute-start(bf16[16,2048]{1,0:T(8,128)(2,1)} %param.12), channel_id=1, source_target_pairs={{0,1},{1,2},{2,3},{3,0},{4,5},{5,6},{6,7},{7,4},{8,9},{9,10},{10,1... | collective-permute-start | bytes 196616 | tf_op jit(solution)/shard_map/ppermute | solution.py:419
  6.8 8.9 %collective-permute-start.7 = (bf16[16,2048]{1,0:T(8,128)(2,1)}, bf16[16,2048]{1,0:T(8,128)(2,1)S(1)}, u32[]{:S(2)}, u32[]{:S(2)}) collective-permute-start(bf16[16,2048]{1,0:T(8,128)(2,1)} %param.12), channel_id=1, source_target_pairs={{0,2},{1,3},{2,0},{3,1},{4,6},{5,7},{6,4},{7,5},{8,10},{9,11},{10,... | collective-permute-start | bytes 196616 | tf_op jit(solution)/shard_map/ppermute | solution.py:419
  8.9 5.6 %copy-start.1 = (bf16[16,2048]{1,0:T(8,128)(2,1)S(1)}, bf16[16,2048]{1,0:T(8,128)(2,1)}, u32[]{:S(2)}) copy-start(bf16[16,2048]{1,0:T(8,128)(2,1)} %param.12) | copy-start | bytes 196612
  14.5 3.2 %collective-permute-start.8 = (bf16[16,2048]{1,0:T(8,128)(2,1)S(1)}, bf16[16,2048]{1,0:T(8,128)(2,1)S(1)}, u32[]{:S(2)}, u32[]{:S(2)}) collective-permute-start(bf16[16,2048]{1,0:T(8,128)(2,1)S(1)} %copy-done.1), channel_id=1, source_target_pairs={{0,3},{1,0},{2,1},{3,2},{4,7},{5,4},{6,5},{7,6},{8,11},{9,8},{10,9... | collective-permute-start | bytes 196616 | tf_op jit(solution)/shard_map/ppermute | solution.py:419
  17.8 14.1 %copy-start = (bf16[1,2,16,3696]{3,2,1,0:T(8,128)(2,1)S(1)}, bf16[1,2,16,3696]{3,2,1,0:T(8,128)(2,1)}, u32[]{:S(2)}) copy-start(bf16[1,2,16,3696]{3,2,1,0:T(8,128)(2,1)} %param.10) | copy-start | bytes 709636
  31.7 28.7 %collective-permute-start.9 = (bf16[1280,2048]{1,0:T(8,128)(2,1)S(1)}, bf16[1280,2048]{1,0:T(8,128)(2,1)S(1)}, u32[]{:S(2)}, u32[]{:S(2)}) collective-permute-start(bf16[1280,2048]{1,0:T(8,128)(2,1)S(1)} %get-tuple-element.36.refs_10_), channel_id=1, source_target_pairs={{0,16},{16,0},{1,17},{17,1},{2,18},{18,2},{3,19},{19,3},{4,20},{20... | collective-permute-start | bytes 15728648 | tf_op jit(solution)/shard_map/ppermute | solution.py:530
  31.9 4.4 %collective-permute-start.3 = (bf16[16,3696]{1,0:T(8,128)(2,1)S(1)}, bf16[16,3696]{1,0:T(8,128)(2,1)S(1)}, u32[]{:S(2)}, u32[]{:S(2)}) collective-permute-start(bf16[16,3696]{1,0:T(8,128)(2,1)S(1)} %fusion.16), channel_id=1, source_target_pairs={{0,4},{4,8},{8,12},{12,0},{1,5},{5,9},{9,13},{13,1},{2,6},{6,10},{... | collective-permute-start | bytes 354824 | tf_op jit(solution)/shard_map/ppermute | solution.py:419
  32.0 10.4 %collective-permute-start.4 = (bf16[16,3696]{1,0:T(8,128)(2,1)S(1)}, bf16[16,3696]{1,0:T(8,128)(2,1)S(1)}, u32[]{:S(2)}, u32[]{:S(2)}) collective-permute-start(bf16[16,3696]{1,0:T(8,128)(2,1)S(1)} %fusion.16), channel_id=1, source_target_pairs={{0,8},{4,12},{8,0},{12,4},{1,9},{5,13},{9,1},{13,5},{2,10},{6,14},... | collective-permute-start | bytes 354824 | tf_op jit(solution)/shard_map/ppermute | solution.py:419
  35.1 10.3 %collective-permute-start.5 = (bf16[16,3696]{1,0:T(8,128)(2,1)S(1)}, bf16[16,3696]{1,0:T(8,128)(2,1)S(1)}, u32[]{:S(2)}, u32[]{:S(2)}) collective-permute-start(bf16[16,3696]{1,0:T(8,128)(2,1)S(1)} %fusion.16), channel_id=1, source_target_pairs={{0,12},{4,0},{8,4},{12,8},{1,13},{5,1},{9,5},{13,9},{2,14},{6,2},{... | collective-permute-start | bytes 354824 | tf_op jit(solution)/shard_map/ppermute | solution.py:419
  45.7 27.2 %collective-permute-start.10 = (bf16[1152,2048]{1,0:T(8,128)(2,1)S(1)}, bf16[1152,2048]{1,0:T(8,128)(2,1)S(1)}, u32[]{:S(2)}, u32[]{:S(2)}) collective-permute-start(bf16[1152,2048]{1,0:T(8,128)(2,1)S(1)} %get-tuple-element.43), channel_id=1, source_target_pairs={{0,16},{16,0},{1,17},{17,1},{2,18},{18,2},{3,19},{19,3},{4,20},{20... | collective-permute-start | bytes 14155784 | tf_op jit(solution)/shard_map/ppermute | solution.py:530
  64.7 15.0 %collective-permute-start.11 = (bf16[896,2048]{1,0:T(8,128)(2,1)}, bf16[896,2048]{1,0:T(8,128)(2,1)}, u32[]{:S(2)}, u32[]{:S(2)}) collective-permute-start(bf16[896,2048]{1,0:T(8,128)(2,1)} %get-tuple-element.47), channel_id=1, source_target_pairs={{0,16},{16,0},{1,17},{17,1},{2,18},{18,2},{3,19},{19,3},{4,20},{20... | collective-permute-start | bytes 11010056 | tf_op jit(solution)/shard_map/ppermute | solution.py:530
  72.9 6.8 %copy-start.3 = (s32[1,16]{1,0:T(1,128)S(1)}, s32[1,16]{1,0:T(1,128)}, u32[]{:S(2)}) copy-start(s32[1,16]{1,0:T(1,128)} %param.16) | copy-start | bytes 196
  76.8 8.0 %collective-permute-start.12 = (bf16[368,2048]{1,0:T(8,128)(2,1)}, bf16[368,2048]{1,0:T(8,128)(2,1)}, u32[]{:S(2)}, u32[]{:S(2)}) collective-permute-start(bf16[368,2048]{1,0:T(8,128)(2,1)} %get-tuple-element.51), channel_id=1, source_target_pairs={{0,16},{16,0},{1,17},{17,1},{2,18},{18,2},{3,19},{19,3},{4,20},{20... | collective-permute-start | bytes 4521992 | tf_op jit(solution)/shard_map/ppermute | solution.py:530
  84.8 5.9 %copy-start.4 = (s32[1,16]{1,0:T(1,128)S(1)}, s32[1,16]{1,0:T(1,128)}, u32[]{:S(2)}) copy-start(s32[1,16]{1,0:T(1,128)} %param.17) | copy-start | bytes 196
  84.8 10.3 %copy-start.2 = (bf16[1,2,16,2048]{3,2,1,0:T(8,128)(2,1)S(1)}, bf16[1,2,16,2048]{3,2,1,0:T(8,128)(2,1)}, u32[]{:S(2)}) copy-start(bf16[1,2,16,2048]{3,2,1,0:T(8,128)(2,1)} %param.11) | copy-start | bytes 393220
  88.0 4.6 %collective-permute-start.13 = (bf16[2,16,2048]{2,1,0:T(8,128)(2,1)S(1)}, bf16[2,16,2048]{2,1,0:T(8,128)(2,1)S(1)}, u32[]{:S(2)}, u32[]{:S(2)}) collective-permute-start(bf16[2,16,2048]{2,1,0:T(8,128)(2,1)S(1)} %get-tuple-element.57), channel_id=1, source_target_pairs={{0,1},{1,0},{2,3},{3,2},{4,5},{5,4},{6,7},{7,6},{8,9},{9,8},{10,11... | collective-permute-start | bytes 393224 | tf_op jit(solution)/shard_map/ppermute | solution.py:443
  89.1 4.3 %collective-permute-start.14 = (bf16[2,16,2048]{2,1,0:T(8,128)(2,1)S(1)}, bf16[2,16,2048]{2,1,0:T(8,128)(2,1)S(1)}, u32[]{:S(2)}, u32[]{:S(2)}) collective-permute-start(bf16[2,16,2048]{2,1,0:T(8,128)(2,1)S(1)} %get-tuple-element.59), channel_id=1, source_target_pairs={{0,2},{1,3},{2,0},{3,1},{4,6},{5,7},{6,4},{7,5},{8,10},{9,11},{10,... | collective-permute-start | bytes 393224 | tf_op jit(solution)/shard_map/ppermute | solution.py:443
  90.4 4.7 %collective-permute-start.15 = (bf16[2,16,2048]{2,1,0:T(8,128)(2,1)S(1)}, bf16[2,16,2048]{2,1,0:T(8,128)(2,1)S(1)}, u32[]{:S(2)}, u32[]{:S(2)}) collective-permute-start(bf16[2,16,2048]{2,1,0:T(8,128)(2,1)S(1)} %get-tuple-element.58), channel_id=1, source_target_pairs={{0,3},{1,2},{2,1},{3,0},{4,7},{5,6},{6,5},{7,4},{8,11},{9,10},{10,... | collective-permute-start | bytes 393224 | tf_op jit(solution)/shard_map/ppermute | solution.py:443

commit v2 on v1

--- a/solution.py
+++ b/solution.py
@@ -30,8 +30,8 @@
 SLOTS = 4
 OUT_SLOTS = 4
 PIECES = 4
-EARLY_TILES = 5
-FAR_CHUNKS = 2
+EARLY_TILES = 4
+FAR_CHUNKS = 0
 STAGE_LIMIT = 22 * 1024 * 1024
 EARLY_LIMIT = 2 * 1024 * 1024
 WIDE = 256
@@ -125,8 +125,15 @@
     got = refs.pop(0) if take else None
     early = [refs.pop(0) for _ in range(3)] if plan["early"] else None
     past = refs.pop(0) if plan["past"] else None
-    acc_one, acc_two, upd = refs[:3]
-    refs = refs[3:]
+    place = refs.pop(0) if plan["final"] else None
+    if plan["final"]:
+        upd = refs.pop(0)
+        acc_one, acc_two = refs[-2:]
+        refs = refs[:-2]
+        own, *pieces = [refs.pop(0) for _ in range(plan["final"])]
+    else:
+        acc_one, acc_two, upd = refs[:3]
+        refs = refs[3:]
     fresh = refs.pop(0) if learn else None
     w_buf, m1_buf, m2_buf, u_buf, b_buf, in_sem, out_sem, b_sem = refs
     width = cot.shape[1]
@@ -317,6 +324,15 @@
         pl.when(role[0] == 1)(rollout_first)
     if take:
         pl.when(role[0] == 1)(rollout_take)
+    if plan["final"]:
+        size = own.shape[1]
+        for which, acc in enumerate((acc_one, acc_two)):
+            for mask in range(plan["final"]):
+                rows = pl.ds(pl.multiple_of((place[0] ^ mask) * size, 8), size)
+                if mask:
+                    pieces[mask - 1][which] = acc[rows, :].astype(jnp.bfloat16)
+                else:
+                    own[which] = acc[rows, :]
 
 
 def early_kernel(w, m1, m2, w_out, m1_out, m2_out, sems):
@@ -346,7 +362,7 @@
     )(w, m1, m2)
 
 
-def stage(plan, role, h, nx, cot, w, m1, m2, state, got, early, past):
+def stage(plan, role, h, nx, cot, w, m1, m2, state, got, early, past, place):
     rows, width = h.shape[0], cot.shape[1]
     height = w.shape[0]
     vmem = pl.BlockSpec(memory_space=pltpu.VMEM)
@@ -369,6 +385,9 @@
     if past is not None:
         args.append(past)
         specs.append(vmem)
+    if plan["final"]:
+        args.append(place)
+        specs.append(pl.BlockSpec(memory_space=pltpu.SMEM))
     out = [
         jax.ShapeDtypeStruct((rows, width), jnp.float32),
         jax.ShapeDtypeStruct((rows, width), jnp.float32),
@@ -381,6 +400,14 @@
         where = pltpu.HBM if plan["far"] else pltpu.VMEM
         out.append(where((span, width), jnp.bfloat16))
         out_specs.append(hbm if plan["far"] else vmem)
+    sums = []
+    if plan["final"]:
+        out, out_specs, alias = out[2:], out_specs[2:], {9: 0}
+        sums = [pltpu.VMEM((rows, width), jnp.float32)] * 2
+        piece = (2, rows // plan["final"], width)
+        out.append(jax.ShapeDtypeStruct(piece, jnp.float32))
+        out += [jax.ShapeDtypeStruct(piece, jnp.bfloat16)] * (plan["final"] - 1)
+        out_specs += [vmem] * plan["final"]
     plan = dict(
         plan,
         carry=state is not None,
@@ -405,7 +432,8 @@
             pltpu.SemaphoreType.DMA((SLOTS, 3)),
             pltpu.SemaphoreType.DMA((OUT_SLOTS,)),
             pltpu.SemaphoreType.DMA((OUT_SLOTS,)),
-        ],
+        ]
+        + sums,
         input_output_aliases=alias,
         compiler_params=pltpu.CompilerParams(vmem_limit_bytes=STAGE_LIMIT),
         cost_estimate=cost,
@@ -430,19 +458,11 @@
     return whole
 
 
-def scatter_sum(partials, axis):
-    size = lax.axis_size(axis)
-    if size > 4 or size & (size - 1):
-        return lax.psum_scatter(partials, axis, scatter_dimension=1, tiled=True)
-    rows = partials.shape[1] // size
-    me = lax.axis_index(axis)
-    total = lax.dynamic_slice_in_dim(partials, me * rows, rows, 1)
-    sent = partials.astype(jnp.bfloat16)
-    for mask in range(1, size):
-        piece = lax.dynamic_slice_in_dim(sent, (me ^ mask) * rows, rows, 1)
-        came = lax.ppermute(piece, axis, [(i, i ^ mask) for i in range(size)])
-        total = total + came.astype(jnp.float32)
-    return total
+def exchange(own, pieces, axis):
+    for mask, piece in enumerate(pieces, 1):
+        size = lax.axis_size(axis)
+        own = own + lax.ppermute(piece, axis, [(i, i ^ mask) for i in range(size)])
+    return own
 
 
 SHARES = (0.36, 0.31, 0.21, 0.12)
@@ -499,6 +519,8 @@
 
     state = None
     made, flying = [], []
+    others = lax.axis_size("tp") - 1 if lax.axis_size("tp") in (2, 4) else 0
+    place = lax.axis_index("tp").astype(jnp.int32).reshape(1)
     for step in range(count + 2):
         far = step >= count - FAR_CHUNKS
         plan = {
@@ -508,6 +530,7 @@
             "second": step > 0,
             "past": chunks[0] if step == 1 else None,
             "far": far,
+            "final": others + 1 if others and step == count + 1 else 0,
             "take_far": step - 2 >= count - FAR_CHUNKS,
         }
         result = stage(
@@ -523,18 +546,23 @@
             flying[step - 2] if step >= 2 else None,
             early if step == 0 else None,
             made[0] if step == 1 else None,
+            place,
         )
         state = tuple(result[:3])
         if step < count:
             made.append(result[3])
             flying.append(lax.ppermute(result[3], "role", [(0, 1), (1, 0)]))
-    sums = scatter_sum(jnp.stack(state[:2]), "tp")
+    if others:
+        new_weights = result[0]
+        sums = exchange(result[1], result[2:], "tp")
+    else:
+        new_weights = state[2]
+        sums = lax.psum_scatter(jnp.stack(state[:2]), "tp", scatter_dimension=1, tiled=True)
     first_sum, next_sum = sums[0], sums[1]
-    new_weights = state[2]
 
     first_out = (stream[0, 0].astype(jnp.float32) + factor * first_sum).astype(jnp.bfloat16)
     block_rows = first_out.shape[0]
-    local_parent = tree_parent[0] - lax.axis_index("tp") * block_rows
+    local_parent = lax.rem(tree_parent[0], jnp.int32(block_rows))
     onehot = (local_parent[:, None] == jnp.arange(block_rows, dtype=jnp.int32)[None, :]).astype(
         jnp.bfloat16
     )

time: 97.1 us -> 93.5 us (0.963)
  the two profiles are of different devices: /device:TPU:9 before, /device:TPU:0 now
where the time goes in v2:
time: 93.5 us; the launch traced here: 92.8 us
  Pallas kernels  48.2 us (52%)
  waiting for transfers between devices  20.6 us (22%)
  starting transfers between devices  19.3 us (21%)
  other arithmetic  1.86 us (2%)
  local copies, waits for them, and re-layouts  1.14 us (1%)
    pallas_call x6, Pallas kernels, stage(): pl.pallas_call(functools.partial(stage_kernel, plan), out_shape=out, in_s...  43.5 us
    ppermute x9, starting transfers between devices, shifts_of(): lax.ppermute(piece, axis, [(i, (i + by) % size) for i in range(size)])  15.4 us
    ppermute x9, waiting for transfers between devices, shifts_of(): lax.ppermute(piece, axis, [(i, (i + by) % size) for i in range(size)])  11.6 us
    ppermute x3, waiting for transfers between devices, exchange(): own = own + lax.ppermute(piece, axis, [(i, i ^ mask) for i in range(size)])  6.05 us
    pallas_call x1, Pallas kernels, fetch_early(): pl.pallas_call(early_kernel, out_shape=[shape] * 3, in_specs=[pl.BlockSpe...  4.65 us
    ppermute x3, starting transfers between devices, exchange(): own = own + lax.ppermute(piece, axis, [(i, i ^ mask) for i in range(size)])  3.55 us
    ppermute x4, waiting for transfers between devices, compute(): flying.append(lax.ppermute(result[3], 'role', [(0, 1), (1, 0)]))  3.01 us
  transfers between devices with their start and end apart: 16, of which 7 were waited for; matrix products, arithmetic and copies ran while one was open for 1% of the time, Pallas kernels for 39%

profile of v2, /device:TPU:0, one launch (start us, length us, event | category | flops | bytes accessed | tf_op | source)
XLA Modules:
  0.0 92.8 jit_solution(16547704989069968757)
XLA Ops:
  0.7 1.1 %constant_dynamic-update-slice_fusion.11 = (bf16[64,3696]{1,0:T(8,128)(2,1)S(1)}, bf16[16,3696]{1,0:T(8,128)(2,1)S(1)}) fusion(bf16[64,3696]{1,0:T(8,128)(2,1)S(1)} %broadcast.49.clone, s32[]{:T(128)S(6)} %select_n.72, bf16[1,2,16,3696]{3,2,1,0:T(8,128)(2,1)} %param.9), kind=kLoop, calls=%fused_computation.44 | loop fusion | flops 473088 | bytes 474116 | tf_op jit(solution)/shard_map/dynamic_update_slice | solution.py:457
  1.7 3.1 %collective-permute-start = (bf16[16,3696]{1,0:T(8,128)(2,1)S(1)}, bf16[16,3696]{1,0:T(8,128)(2,1)S(1)}, u32[]{:S(2)}, u32[]{:S(2)}) collective-permute-start(bf16[16,3696]{1,0:T(8,128)(2,1)S(1)} %get-tuple-element.60), channel_id=1, source_target_pairs={{0,4},{4,8},{8,12},{12,0},{1,5},{5,9},{9,13},{13,1},{2,6},{6,10},{... | collective-permute-start | bytes 354824 | tf_op jit(solution)/shard_map/ppermute | solution.py:447
  4.8 2.6 %collective-permute-start.1 = (bf16[16,3696]{1,0:T(8,128)(2,1)S(1)}, bf16[16,3696]{1,0:T(8,128)(2,1)S(1)}, u32[]{:S(2)}, u32[]{:S(2)}) collective-permute-start(bf16[16,3696]{1,0:T(8,128)(2,1)S(1)} %get-tuple-element.60), channel_id=1, source_target_pairs={{0,8},{4,12},{8,0},{12,4},{1,9},{5,13},{9,1},{13,5},{2,10},{6,14},... | collective-permute-start | bytes 354824 | tf_op jit(solution)/shard_map/ppermute | solution.py:447
  7.4 1.3 %collective-permute-start.2 = (bf16[16,3696]{1,0:T(8,128)(2,1)S(1)}, bf16[16,3696]{1,0:T(8,128)(2,1)S(1)}, u32[]{:S(2)}, u32[]{:S(2)}) collective-permute-start(bf16[16,3696]{1,0:T(8,128)(2,1)S(1)} %get-tuple-element.60), channel_id=1, source_target_pairs={{0,12},{4,0},{8,4},{12,8},{1,13},{5,1},{9,5},{13,9},{2,14},{6,2},{... | collective-permute-start | bytes 354824 | tf_op jit(solution)/shard_map/ppermute | solution.py:447
  8.8 1.5 %collective-permute-start.6 = (bf16[16,2048]{1,0:T(8,128)(2,1)}, bf16[16,2048]{1,0:T(8,128)(2,1)S(1)}, u32[]{:S(2)}, u32[]{:S(2)}) collective-permute-start(bf16[16,2048]{1,0:T(8,128)(2,1)} %param.12), channel_id=1, source_target_pairs={{0,1},{1,2},{2,3},{3,0},{4,5},{5,6},{6,7},{7,4},{8,9},{9,10},{10,1... | collective-permute-start | bytes 196616 | tf_op jit(solution)/shard_map/ppermute | solution.py:447
  10.3 1.5 %collective-permute-start.7 = (bf16[16,2048]{1,0:T(8,128)(2,1)}, bf16[16,2048]{1,0:T(8,128)(2,1)S(1)}, u32[]{:S(2)}, u32[]{:S(2)}) collective-permute-start(bf16[16,2048]{1,0:T(8,128)(2,1)} %param.12), channel_id=1, source_target_pairs={{0,2},{1,3},{2,0},{3,1},{4,6},{5,7},{6,4},{7,5},{8,10},{9,11},{10,... | collective-permute-start | bytes 196616 | tf_op jit(solution)/shard_map/ppermute | solution.py:447
  11.8 0.9 constant_dynamic-update-slice_fusion.3
  12.7 0.0 copy-start.1
  12.7 4.6 %shard_map.112 = (f32[512,2048]{1,0:T(8,128)S(1)}, f32[512,2048]{1,0:T(8,128)S(1)}, f32[512,2048]{1,0:T(8,128)S(1)}) custom-call(f32[3696,2048]{1,0:T(8,128)} %bitcast.49, f32[3696,2048]{1,0:T(8,128)} %refs_5_.11, f32[3696,2048]{1,0:T(8,128)} %refs_6_.11), custom_call_target="tpu_custom_call" | custom-call | flops 201326592 | bytes 25165824 | tf_op jit(solution)/shard_map/pallas_call | solution.py:354
  17.3 0.0 collective-permute-done.6
  17.3 0.0 copy-done.1
  17.4 1.5 %collective-permute-start.8 = (bf16[16,2048]{1,0:T(8,128)(2,1)S(1)}, bf16[16,2048]{1,0:T(8,128)(2,1)S(1)}, u32[]{:S(2)}, u32[]{:S(2)}) collective-permute-start(bf16[16,2048]{1,0:T(8,128)(2,1)S(1)} %copy-done.1), channel_id=1, source_target_pairs={{0,3},{1,0},{2,1},{3,2},{4,7},{5,4},{6,5},{7,6},{8,11},{9,8},{10,9... | collective-permute-start | bytes 196616 | tf_op jit(solution)/shard_map/ppermute | solution.py:447
  18.8 0.0 collective-permute-done.7
  18.9 2.8 %collective-permute-done.8 = bf16[16,2048]{1,0:T(8,128)(2,1)S(1)} collective-permute-done((bf16[16,2048]{1,0:T(8,128)(2,1)S(1)}, bf16[16,2048]{1,0:T(8,128)(2,1)S(1)}, u32[]{:S(2)}, u32[]{:S(2)}) %collective-permute-start.8) | collective-permute-done | bytes 65568 | tf_op jit(solution)/shard_map/ppermute | solution.py:447
  21.7 0.0 collective-permute-done
  21.7 0.0 collective-permute-done.1
  21.8 0.0 collective-permute-done.2
  21.8 0.0 copy-start
  21.8 11.3 %shard_map.113 = (f32[64,2048]{1,0:T(8,128)S(1)}, f32[64,2048]{1,0:T(8,128)S(1)}, f32[3696,2048]{1,0:T(8,128)}, bf16[1280,2048]{1,0:T(8,128)(2,1)S(1)}) custom-call(s32[1]{0:T(128)} %bitcast.1.refs_0_, bf16[64,3696]{1,0:T(8,128)(2,1)S(1)} %constant_dynamic-update-slice_fusion.8.refs_1_.refs_2_, ...), custom_call_target="tpu_custom_call" | custom-call | flops 1009632960 | bytes 53428800 | tf_op jit(solution)/shard_map/pallas_call | solution.py:421
  33.1 0.1 collective-permute-start.9
  33.2 0.0 copy-done
  33.2 0.1 fusion.11
  33.3 0.7 collective-permute-start.3
  34.0 0.3 collective-permute-start.4
  34.4 2.8 %collective-permute-start.5 = (bf16[16,3696]{1,0:T(8,128)(2,1)S(1)}, bf16[16,3696]{1,0:T(8,128)(2,1)S(1)}, u32[]{:S(2)}, u32[]{:S(2)}) collective-permute-start(bf16[16,3696]{1,0:T(8,128)(2,1)S(1)} %fusion.11), channel_id=1, source_target_pairs={{0,12},{4,0},{8,4},{12,8},{1,13},{5,1},{9,5},{13,9},{2,14},{6,2},{... | collective-permute-start | bytes 354824 | tf_op jit(solution)/shard_map/ppermute | solution.py:447
  37.2 4.2 %collective-permute-done.3 = bf16[16,3696]{1,0:T(8,128)(2,1)S(1)} collective-permute-done((bf16[16,3696]{1,0:T(8,128)(2,1)S(1)}, bf16[16,3696]{1,0:T(8,128)(2,1)S(1)}, u32[]{:S(2)}, u32[]{:S(2)}) %collective-permute-start.3) | collective-permute-done | bytes 118304 | tf_op jit(solution)/shard_map/ppermute | solution.py:447
  41.4 4.6 %collective-permute-done.4 = bf16[16,3696]{1,0:T(8,128)(2,1)S(1)} collective-permute-done((bf16[16,3696]{1,0:T(8,128)(2,1)S(1)}, bf16[16,3696]{1,0:T(8,128)(2,1)S(1)}, u32[]{:S(2)}, u32[]{:S(2)}) %collective-permute-start.4) | collective-permute-done | bytes 118304 | tf_op jit(solution)/shard_map/ppermute | solution.py:447
  46.0 0.0 collective-permute-done.5
  46.0 13.9 %shard_map.114 = (f32[64,2048]{1,0:T(8,128)S(1)}, f32[64,2048]{1,0:T(8,128)S(1)}, f32[3696,2048]{1,0:T(8,128)}, bf16[1152,2048]{1,0:T(8,128)(2,1)S(1)}) custom-call(s32[1]{0:T(128)} %bitcast.1.refs_0_, bf16[64,3696]{1,0:T(8,128)(2,1)S(1)} %constant_dynamic-update-slice_fusion.8.refs_1_.refs_2_, ...), custom_call_target="tpu_custom_call", output_to_operand_aliasing={{2}: (9, {})} | custom-call | flops 908969664 | bytes 48185920 | tf_op jit(solution)/shard_map/pallas_call | solution.py:421
  59.9 0.1 collective-permute-start.10
  60.0 0.0 collective-permute-done.9.refs_10_
  60.0 11.3 %shard_map.115 = (f32[64,2048]{1,0:T(8,128)S(1)}, f32[64,2048]{1,0:T(8,128)S(1)}, f32[3696,2048]{1,0:T(8,128)}, bf16[896,2048]{1,0:T(8,128)(2,1)S(1)}) custom-call(s32[1]{0:T(128)} %bitcast.1.refs_0_, bf16[64,3696]{1,0:T(8,128)(2,1)S(1)} %constant_dynamic-update-slice_fusion.8.refs_1_.refs_2_, ...), custom_call_target="tpu_custom_call", output_to_operand_aliasing={{2}: (9, {})} | custom-call | flops 707643072 | bytes 37700160 | tf_op jit(solution)/shard_map/pallas_call | solution.py:421
  71.3 0.1 collective-permute-start.11
  71.4 0.0 collective-permute-done.10.refs_10_
  71.4 0.0 copy-start.3
  71.4 6.5 %shard_map.116 = (f32[64,2048]{1,0:T(8,128)S(1)}, f32[64,2048]{1,0:T(8,128)S(1)}, f32[3696,2048]{1,0:T(8,128)}, bf16[368,2048]{1,0:T(8,128)(2,1)S(1)}) custom-call(s32[1]{0:T(128)} %bitcast.1.refs_0_, bf16[64,3696]{1,0:T(8,128)(2,1)S(1)} %constant_dynamic-update-slice_fusion.8.refs_1_.refs_2_, ...), custom_call_target="tpu_custom_call", output_to_operand_aliasing={{2}: (9, {})} | custom-call | flops 292406976 | bytes 16073280 | tf_op jit(solution)/shard_map/pallas_call | solution.py:421
  77.9 0.1 collective-permute-start.12
  78.0 0.0 copy-done.3
  78.0 0.0 collective-permute-done.11.refs_10_
  78.0 0.3 shard_map.117
  78.3 3.0 %collective-permute-done.12.refs_10_ = bf16[368,2048]{1,0:T(8,128)(2,1)S(1)} collective-permute-done((bf16[368,2048]{1,0:T(8,128)(2,1)S(1)}, bf16[368,2048]{1,0:T(8,128)(2,1)S(1)}, u32[]{:S(2)}, u32[]{:S(2)}) %collective-permute-start.12) | collective-permute-done | bytes 1507360 | tf_op jit(solution)/shard_map/ppermute | solution.py:554
  81.3 0.0 copy-start.4
  81.3 0.0 copy-start.2
  81.3 0.3 shard_map.118
  81.6 1.4 %collective-permute-start.13 = (bf16[2,16,2048]{2,1,0:T(8,128)(2,1)S(1)}, bf16[2,16,2048]{2,1,0:T(8,128)(2,1)S(1)}, u32[]{:S(2)}, u32[]{:S(2)}) collective-permute-start(bf16[2,16,2048]{2,1,0:T(8,128)(2,1)S(1)} %get-tuple-element.55), channel_id=1, source_target_pairs={{0,1},{1,0},{2,3},{3,2},{4,5},{5,4},{6,7},{7,6},{8,9},{9,8},{10,11... | collective-permute-start | bytes 393224 | tf_op jit(solution)/shard_map/ppermute | solution.py:464
  83.1 1.5 %collective-permute-start.14 = (bf16[2,16,2048]{2,1,0:T(8,128)(2,1)S(1)}, bf16[2,16,2048]{2,1,0:T(8,128)(2,1)S(1)}, u32[]{:S(2)}, u32[]{:S(2)}) collective-permute-start(bf16[2,16,2048]{2,1,0:T(8,128)(2,1)S(1)} %get-tuple-element.56), channel_id=1, source_target_pairs={{0,2},{1,3},{2,0},{3,1},{4,6},{5,7},{6,4},{7,5},{8,10},{9,11},{10,... | collective-permute-start | bytes 393224 | tf_op jit(solution)/shard_map/ppermute | solution.py:464
  84.6 0.6 collective-permute-start.15
  85.2 0.0 copy-done.4
  85.2 1.6 %collective-permute-done.13 = bf16[2,16,2048]{2,1,0:T(8,128)(2,1)S(1)} collective-permute-done((bf16[2,16,2048]{2,1,0:T(8,128)(2,1)S(1)}, bf16[2,16,2048]{2,1,0:T(8,128)(2,1)S(1)}, u32[]{:S(2)}, u32[]{:S(2)}) %collective-permute-start.13) | collective-permute-done | bytes 131104 | tf_op jit(solution)/shard_map/ppermute | solution.py:464
  86.8 1.7 %collective-permute-done.14 = bf16[2,16,2048]{2,1,0:T(8,128)(2,1)S(1)} collective-permute-done((bf16[2,16,2048]{2,1,0:T(8,128)(2,1)S(1)}, bf16[2,16,2048]{2,1,0:T(8,128)(2,1)S(1)}, u32[]{:S(2)}, u32[]{:S(2)}) %collective-permute-start.14) | collective-permute-done | bytes 131104 | tf_op jit(solution)/shard_map/ppermute | solution.py:464
  88.4 2.8 %collective-permute-done.15 = bf16[2,16,2048]{2,1,0:T(8,128)(2,1)S(1)} collective-permute-done((bf16[2,16,2048]{2,1,0:T(8,128)(2,1)S(1)}, bf16[2,16,2048]{2,1,0:T(8,128)(2,1)S(1)}, u32[]{:S(2)}, u32[]{:S(2)}) %collective-permute-start.15) | collective-permute-done | bytes 131104 | tf_op jit(solution)/shard_map/ppermute | solution.py:464
  91.2 0.1 convert_add_fusion
  91.3 0.0 copy-done.2
  91.3 0.6 fusion.14
  92.0 0.8 fusion.2
  (15 shorter events, 0.3 us)
Async XLA Ops:
  1.7 19.9 %collective-permute-start = (bf16[16,3696]{1,0:T(8,128)(2,1)S(1)}, bf16[16,3696]{1,0:T(8,128)(2,1)S(1)}, u32[]{:S(2)}, u32[]{:S(2)}) collective-permute-start(bf16[16,3696]{1,0:T(8,128)(2,1)S(1)} %get-tuple-element.60), channel_id=1, source_target_pairs={{0,4},{4,8},{8,12},{12,0},{1,5},{5,9},{9,13},{13,1},{2,6},{6,10},{... | collective-permute-start | bytes 354824 | tf_op jit(solution)/shard_map/ppermute | solution.py:447
  4.8 16.9 %collective-permute-start.1 = (bf16[16,3696]{1,0:T(8,128)(2,1)S(1)}, bf16[16,3696]{1,0:T(8,128)(2,1)S(1)}, u32[]{:S(2)}, u32[]{:S(2)}) collective-permute-start(bf16[16,3696]{1,0:T(8,128)(2,1)S(1)} %get-tuple-element.60), channel_id=1, source_target_pairs={{0,8},{4,12},{8,0},{12,4},{1,9},{5,13},{9,1},{13,5},{2,10},{6,14},... | collective-permute-start | bytes 354824 | tf_op jit(solution)/shard_map/ppermute | solution.py:447
  7.4 14.3 %collective-permute-start.2 = (bf16[16,3696]{1,0:T(8,128)(2,1)S(1)}, bf16[16,3696]{1,0:T(8,128)(2,1)S(1)}, u32[]{:S(2)}, u32[]{:S(2)}) collective-permute-start(bf16[16,3696]{1,0:T(8,128)(2,1)S(1)} %get-tuple-element.60), channel_id=1, source_target_pairs={{0,12},{4,0},{8,4},{12,8},{1,13},{5,1},{9,5},{13,9},{2,14},{6,2},{... | collective-permute-start | bytes 354824 | tf_op jit(solution)/shard_map/ppermute | solution.py:447
  8.8 8.5 %collective-permute-start.6 = (bf16[16,2048]{1,0:T(8,128)(2,1)}, bf16[16,2048]{1,0:T(8,128)(2,1)S(1)}, u32[]{:S(2)}, u32[]{:S(2)}) collective-permute-start(bf16[16,2048]{1,0:T(8,128)(2,1)} %param.12), channel_id=1, source_target_pairs={{0,1},{1,2},{2,3},{3,0},{4,5},{5,6},{6,7},{7,4},{8,9},{9,10},{10,1... | collective-permute-start | bytes 196616 | tf_op jit(solution)/shard_map/ppermute | solution.py:447
  10.3 8.6 %collective-permute-start.7 = (bf16[16,2048]{1,0:T(8,128)(2,1)}, bf16[16,2048]{1,0:T(8,128)(2,1)S(1)}, u32[]{:S(2)}, u32[]{:S(2)}) collective-permute-start(bf16[16,2048]{1,0:T(8,128)(2,1)} %param.12), channel_id=1, source_target_pairs={{0,2},{1,3},{2,0},{3,1},{4,6},{5,7},{6,4},{7,5},{8,10},{9,11},{10,... | collective-permute-start | bytes 196616 | tf_op jit(solution)/shard_map/ppermute | solution.py:447
  12.7 4.7 %copy-start.1 = (bf16[16,2048]{1,0:T(8,128)(2,1)S(1)}, bf16[16,2048]{1,0:T(8,128)(2,1)}, u32[]{:S(2)}) copy-start(bf16[16,2048]{1,0:T(8,128)(2,1)} %param.12) | copy-start | bytes 196612
  17.4 4.3 %collective-permute-start.8 = (bf16[16,2048]{1,0:T(8,128)(2,1)S(1)}, bf16[16,2048]{1,0:T(8,128)(2,1)S(1)}, u32[]{:S(2)}, u32[]{:S(2)}) collective-permute-start(bf16[16,2048]{1,0:T(8,128)(2,1)S(1)} %copy-done.1), channel_id=1, source_target_pairs={{0,3},{1,0},{2,1},{3,2},{4,7},{5,4},{6,5},{7,6},{8,11},{9,8},{10,9... | collective-permute-start | bytes 196616 | tf_op jit(solution)/shard_map/ppermute | solution.py:447
  21.8 11.4 %copy-start = (bf16[1,2,16,3696]{3,2,1,0:T(8,128)(2,1)S(1)}, bf16[1,2,16,3696]{3,2,1,0:T(8,128)(2,1)}, u32[]{:S(2)}) copy-start(bf16[1,2,16,3696]{3,2,1,0:T(8,128)(2,1)} %param.10) | copy-start | bytes 709636
  33.1 26.9 %collective-permute-start.9 = (bf16[1280,2048]{1,0:T(8,128)(2,1)S(1)}, bf16[1280,2048]{1,0:T(8,128)(2,1)S(1)}, u32[]{:S(2)}, u32[]{:S(2)}) collective-permute-start(bf16[1280,2048]{1,0:T(8,128)(2,1)S(1)} %get-tuple-element.38.refs_10_), channel_id=1, source_target_pairs={{0,16},{16,0},{1,17},{17,1},{2,18},{18,2},{3,19},{19,3},{4,20},{20... | collective-permute-start | bytes 15728648 | tf_op jit(solution)/shard_map/ppermute | solution.py:554
  33.3 8.1 %collective-permute-start.3 = (bf16[16,3696]{1,0:T(8,128)(2,1)S(1)}, bf16[16,3696]{1,0:T(8,128)(2,1)S(1)}, u32[]{:S(2)}, u32[]{:S(2)}) collective-permute-start(bf16[16,3696]{1,0:T(8,128)(2,1)S(1)} %fusion.11), channel_id=1, source_target_pairs={{0,4},{4,8},{8,12},{12,0},{1,5},{5,9},{9,13},{13,1},{2,6},{6,10},{... | collective-permute-start | bytes 354824 | tf_op jit(solution)/shard_map/ppermute | solution.py:447
  34.0 12.0 %collective-permute-start.4 = (bf16[16,3696]{1,0:T(8,128)(2,1)S(1)}, bf16[16,3696]{1,0:T(8,128)(2,1)S(1)}, u32[]{:S(2)}, u32[]{:S(2)}) collective-permute-start(bf16[16,3696]{1,0:T(8,128)(2,1)S(1)} %fusion.11), channel_id=1, source_target_pairs={{0,8},{4,12},{8,0},{12,4},{1,9},{5,13},{9,1},{13,5},{2,10},{6,14},... | collective-permute-start | bytes 354824 | tf_op jit(solution)/shard_map/ppermute | solution.py:447
  34.4 11.6 %collective-permute-start.5 = (bf16[16,3696]{1,0:T(8,128)(2,1)S(1)}, bf16[16,3696]{1,0:T(8,128)(2,1)S(1)}, u32[]{:S(2)}, u32[]{:S(2)}) collective-permute-start(bf16[16,3696]{1,0:T(8,128)(2,1)S(1)} %fusion.11), channel_id=1, source_target_pairs={{0,12},{4,0},{8,4},{12,8},{1,13},{5,1},{9,5},{13,9},{2,14},{6,2},{... | collective-permute-start | bytes 354824 | tf_op jit(solution)/shard_map/ppermute | solution.py:447
  59.9 11.5 %collective-permute-start.10 = (bf16[1152,2048]{1,0:T(8,128)(2,1)S(1)}, bf16[1152,2048]{1,0:T(8,128)(2,1)S(1)}, u32[]{:S(2)}, u32[]{:S(2)}) collective-permute-start(bf16[1152,2048]{1,0:T(8,128)(2,1)S(1)} %get-tuple-element.45), channel_id=1, source_target_pairs={{0,16},{16,0},{1,17},{17,1},{2,18},{18,2},{3,19},{19,3},{4,20},{20... | collective-permute-start | bytes 14155784 | tf_op jit(solution)/shard_map/ppermute | solution.py:554
  71.3 6.7 %collective-permute-start.11 = (bf16[896,2048]{1,0:T(8,128)(2,1)S(1)}, bf16[896,2048]{1,0:T(8,128)(2,1)S(1)}, u32[]{:S(2)}, u32[]{:S(2)}) collective-permute-start(bf16[896,2048]{1,0:T(8,128)(2,1)S(1)} %get-tuple-element.49), channel_id=1, source_target_pairs={{0,16},{16,0},{1,17},{17,1},{2,18},{18,2},{3,19},{19,3},{4,20},{20... | collective-permute-start | bytes 11010056 | tf_op jit(solution)/shard_map/ppermute | solution.py:554
  71.4 6.6 %copy-start.3 = (s32[1,16]{1,0:T(1,128)S(1)}, s32[1,16]{1,0:T(1,128)}, u32[]{:S(2)}) copy-start(s32[1,16]{1,0:T(1,128)} %param.16) | copy-start | bytes 196
  77.9 3.4 %collective-permute-start.12 = (bf16[368,2048]{1,0:T(8,128)(2,1)S(1)}, bf16[368,2048]{1,0:T(8,128)(2,1)S(1)}, u32[]{:S(2)}, u32[]{:S(2)}) collective-permute-start(bf16[368,2048]{1,0:T(8,128)(2,1)S(1)} %get-tuple-element.53), channel_id=1, source_target_pairs={{0,16},{16,0},{1,17},{17,1},{2,18},{18,2},{3,19},{19,3},{4,20},{20... | collective-permute-start | bytes 4521992 | tf_op jit(solution)/shard_map/ppermute | solution.py:554
  81.3 3.9 %copy-start.4 = (s32[1,16]{1,0:T(1,128)S(1)}, s32[1,16]{1,0:T(1,128)}, u32[]{:S(2)}) copy-start(s32[1,16]{1,0:T(1,128)} %param.17) | copy-start | bytes 196
  81.3 10.0 %copy-start.2 = (bf16[1,2,16,2048]{3,2,1,0:T(8,128)(2,1)S(1)}, bf16[1,2,16,2048]{3,2,1,0:T(8,128)(2,1)}, u32[]{:S(2)}) copy-start(bf16[1,2,16,2048]{3,2,1,0:T(8,128)(2,1)} %param.11) | copy-start | bytes 393220
  81.6 5.2 %collective-permute-start.13 = (bf16[2,16,2048]{2,1,0:T(8,128)(2,1)S(1)}, bf16[2,16,2048]{2,1,0:T(8,128)(2,1)S(1)}, u32[]{:S(2)}, u32[]{:S(2)}) collective-permute-start(bf16[2,16,2048]{2,1,0:T(8,128)(2,1)S(1)} %get-tuple-element.55), channel_id=1, source_target_pairs={{0,1},{1,0},{2,3},{3,2},{4,5},{5,4},{6,7},{7,6},{8,9},{9,8},{10,11... | collective-permute-start | bytes 393224 | tf_op jit(solution)/shard_map/ppermute | solution.py:464
  83.1 5.4 %collective-permute-start.14 = (bf16[2,16,2048]{2,1,0:T(8,128)(2,1)S(1)}, bf16[2,16,2048]{2,1,0:T(8,128)(2,1)S(1)}, u32[]{:S(2)}, u32[]{:S(2)}) collective-permute-start(bf16[2,16,2048]{2,1,0:T(8,128)(2,1)S(1)} %get-tuple-element.56), channel_id=1, source_target_pairs={{0,2},{1,3},{2,0},{3,1},{4,6},{5,7},{6,4},{7,5},{8,10},{9,11},{10,... | collective-permute-start | bytes 393224 | tf_op jit(solution)/shard_map/ppermute | solution.py:464
  84.6 6.7 %collective-permute-start.15 = (bf16[2,16,2048]{2,1,0:T(8,128)(2,1)S(1)}, bf16[2,16,2048]{2,1,0:T(8,128)(2,1)S(1)}, u32[]{:S(2)}, u32[]{:S(2)}) collective-permute-start(bf16[2,16,2048]{2,1,0:T(8,128)(2,1)S(1)} %get-tuple-element.57), channel_id=1, source_target_pairs={{0,3},{1,2},{2,1},{3,0},{4,7},{5,6},{6,5},{7,4},{8,11},{9,10},{10,... | collective-permute-start | bytes 393224 | tf_op jit(solution)/shard_map/ppermute | solution.py:464
